TPU v7x, 32 devices: a whole 2x2x4 slice. The times are simulated.
32 devices in a mesh: col: 8 (over z, y), row: 4 (over x, core).
Axes of the slice: x: 2, y: 2, z: 4, core: 2. Of those that a mesh axis runs over, the one named last changes fastest.
Arguments:
- vel_u: float32 [75, 192, 2048], P(None, 'row', 'col')
- vel_v: float32 [75, 192, 2048], P(None, 'row', 'col')
- temperature: float32 [75, 192, 2048], P(None, 'row', 'col')
- salinity: float32 [75, 192, 2048], P(None, 'row', 'col')
- sea_level: float32 [192, 2048], P('row', 'col')
- trans_u: float32 [192, 2048], P('row', 'col')
- trans_v: float32 [192, 2048], P('row', 'col')
- bathymetry: float32 [192, 2048], P('row', 'col')
- kmt_levels: int32 [192, 2048], P('row', 'col')
- tide_force: float32 [30, 2], replicated
Outputs:
- output 1: float32 [192, 2048], P('row', 'col')
- output 2: float32 [192, 2048], P('row', 'col')
- output 3: float32 [192, 2048], P('row', 'col')
- output 4: float32 [75, 192, 2048], P(None, 'row', 'col')
- output 5: float32 [75, 192, 2048], P(None, 'row', 'col')
- output 6: float32 [75, 192, 2048], P(None, 'row', 'col')
- output 7: float32 [75, 192, 2048], P(None, 'row', 'col')
All inputs are finite; a program needn't handle non-finite values.
Results may differ from a plain program's by a relative error of at most 0.001.
Values sent between devices are 32-bit elements.
A program may use at most 1 GiB of HBM per device.

v0:
```python
import functools

import jax
import jax.numpy as jnp
from jax import lax
from jax.experimental import pallas as pl
from jax.experimental.pallas import tpu as pltpu
from jax.sharding import PartitionSpec as P

TIME_STEP = 4.0
ALPHA_T = 0.02
BETA_S = 0.015
VISC_KV = 0.001
DIFF_KT = 0.0005
MESH = pl.DeviceIdType.MESH
H = 32
CH = 15
UN = 5
UM = 3
KB = 5
SUB, LANES = 8, 128
LAST = LANES - 1
F32 = jnp.float32
KMT, DEPTH, ETA, TU, TV, FX, FY = range(7)
KU, KV, DZU, DZV, GU, GV, BU, BV, WD = range(9)
FIRST, SECOND = slice(0, 1), slice(1, 2)


def iota(shape, axis):
    return lax.broadcasted_iota(jnp.int32, shape, axis)


def reduced(x):
    return pl.reciprocal(x, approx=False)


def lane_of(x):
    return iota(x.shape, 1)


def slot_of(k, bank):
    b = (k >= bank).astype(jnp.int32)
    return b, 2 * (k - b * bank)


def turn(x, n):
    return pltpu.roll(x, n % LANES if isinstance(n, int) else n, 1)


def shift_east(x, halo):
    left, right = turn(x[:, :LANES], -1), turn(x[:, LANES:], -1)
    edge = lane_of(left) == LAST
    return jnp.concatenate([jnp.where(edge, right, left), jnp.where(edge, halo, right)], axis=1)


def shift_west(x, halo):
    left, right = turn(x[:, :LANES], 1), turn(x[:, LANES:], 1)
    edge = lane_of(left) == 0
    return jnp.concatenate([jnp.where(edge, halo, left), jnp.where(edge, left, right)], axis=1)


def tiles_of(x):
    return [x[SUB * t:SUB * t + SUB] for t in range(x.shape[0] // SUB)]


def shift_north(x, halo):
    rolled = [pltpu.roll(t, SUB - 1, 0) for t in tiles_of(x)]
    edge = iota(rolled[0].shape, 0) == SUB - 1
    rolled.append(jnp.broadcast_to(halo, rolled[0].shape))
    return jnp.concatenate([jnp.where(edge, b, a) for a, b in zip(rolled[:-1], rolled[1:])], axis=0)


def shift_south(x, halo):
    rolled = [pltpu.roll(t, 1, 0) for t in tiles_of(x)]
    edge = iota(rolled[0].shape, 0) == 0
    rolled.insert(0, jnp.broadcast_to(halo, rolled[0].shape))
    return jnp.concatenate([jnp.where(edge, a, b) for a, b in zip(rolled[:-1], rolled[1:])], axis=0)


def merged(west, east):
    even = lane_of(west) % 2 == 0
    back = turn(east, -1)
    return jnp.where(even, west, back), turn(jnp.where(even, back, west), -1)


def main_kernel(n_rows, n_cols,
                kmt_in, bat_in, eta_in, tu_in, tv_in, u_in, v_in, t_in, s_in, tide,
                us_out, vs_out, tm_out, sm_out, bar_out, corr_out, face_out, vcs_out,
                halo_out, trow_n_out, trow_s_out,
                kmt_v, ext, xp, acc, pk_w, pk_e, r_e, r_w, r_ne, r_nw, r_se, r_sw,
                ub, vb, tb, sb, pu, pv, gc, gu, gv, pp, wet_v, dz_v, cc_v, cum_v, faces, coefs, push_v, sum_v,
                bank_uv, bank_ts, sc_w, sc_e, rc_e, rc_w, rc_nw, rc_se, hc, corner_p,
                sr_n, sr_s, sp_s, rr_n, rr_s, rp_n,
                tc_w, tc_e, tr_n, tr_s, qc_e, qc_w, qr_n, qr_s, su_e, sv_n, ru_w, rv_s,
                plane_sem, in_sem, out_sem, send_sem, recv_sem):
    n_sub = tide.shape[0]
    n_lev = u_in.shape[0]
    n_chunk = n_lev // CH
    bank = (n_lev + 1) // 2
    ny, nx = kmt_in.shape
    dt_sub = TIME_STEP / n_sub
    col, row = lax.axis_index("col"), lax.axis_index("row")
    east, west = lax.rem(col + 1, n_cols), lax.rem(col + n_cols - 1, n_cols)
    north, south = lax.rem(row + 1, n_rows), lax.rem(row + n_rows - 1, n_rows)
    where_to = {"n": (col, north), "s": (col, south), "e": (east, row), "w": (west, row),
                "ne": (east, north), "nw": (west, north), "se": (east, south), "sw": (west, south)}
    own = (pl.ds(H, ny), pl.ds(0, nx))
    mid, cols = slice(H, H + ny), slice(0, nx)
    at_n, at_s = slice(H + ny, H + ny + 1), slice(H - 1, H)
    whole, wide = ny + 2 * H, nx + LANES
    at_w, at_e = slice(wide - 1, wide), slice(nx, nx + 1)
    first_row, last_row = FIRST, slice(ny - 1, ny)

    planes = [pltpu.make_async_copy(kmt_in, kmt_v, plane_sem.at[KMT])]
    for i, ref in ((DEPTH, bat_in), (ETA, eta_in), (TU, tu_in), (TV, tv_in)):
        planes.append(pltpu.make_async_copy(ref, ext.at[(i, *own)], plane_sem.at[i]))
    for c in planes:
        c.start()

    def load(a, c):
        src, dst, off = ((t_in, tb, 1), (s_in, sb, 1), (u_in, ub, 0), (v_in, vb, 0))[a]
        return pltpu.make_async_copy(src.at[pl.ds(c * CH, CH)], dst.at[pl.ds(c * CH + off, CH)], in_sem.at[a, c])

    for c in range(n_chunk):
        for a in range(4):
            load(a, c).start()

    barrier = pltpu.get_barrier_semaphore()
    for c_id, r_id in where_to.values():
        pl.semaphore_signal(barrier, inc=1, device_id={"col": c_id, "row": r_id}, device_id_type=MESH)

    used = []

    def remote(src, dst, to):
        c_id, r_id = where_to[to]
        i = len(used)
        used.append(i)
        return pltpu.make_async_remote_copy(src_ref=src, dst_ref=dst, send_sem=send_sem.at[i], recv_sem=recv_sem.at[i],
                                            device_id={"col": c_id, "row": r_id}, device_id_type=MESH)

    def started(copies):
        for c in copies:
            c.start()
        return copies

    def wide_copies(p0, n):
        ps = pl.ds(p0, n)
        low, mids, high = pl.ds(0, 2 * SUB), pl.ds(0, SUB), pl.ds(2 * SUB, SUB)
        return started([
            remote(ext.at[ps, pl.ds(H, H), pl.ds(0, nx)], ext.at[ps, pl.ds(H + ny, H), pl.ds(0, nx)], "s"),
            remote(ext.at[ps, pl.ds(ny, H), pl.ds(0, nx)], ext.at[ps, pl.ds(0, H), pl.ds(0, nx)], "n"),
            remote(pk_w.at[ps, low], r_e.at[ps], "w"),
            remote(pk_e.at[ps, low], r_w.at[ps], "e"),
            remote(pk_w.at[ps, mids], r_ne.at[ps], "sw"),
            remote(pk_e.at[ps, mids], r_nw.at[ps], "se"),
            remote(pk_w.at[ps, high], r_se.at[ps], "nw"),
            remote(pk_e.at[ps, high], r_sw.at[ps], "ne"),
        ])

    group = iota((SUB, LANES), 1) // H
    n_groups = LANES // H

    def pack(p):
        x = ext[(p, *own)]
        for ref, tile, g0 in ((pk_w, x[:, :LANES], 0), (pk_e, x[:, nx - LANES:], n_groups - 1)):
            for at, first, count in ((0, 0, 4), (1, 4, 2), (2, 2, 4)):
                total = jnp.zeros((SUB, LANES), F32)
                for q in range(count):
                    rows = tile[SUB * (first + q):SUB * (first + q) + SUB]
                    rows = turn(rows, H * (q - g0)) if q != g0 else rows
                    total = jnp.where(group == q, rows, total)
                ref[p, SUB * at:SUB * at + SUB, :] = total

    def unpack(p):
        edge = H // SUB
        for t in range(whole // SUB):
            if t < edge:
                e_tile, w_tile, q = r_se[p], r_sw[p], t
            elif t < (H + ny) // SUB:
                rows = slice(SUB * ((t - edge) // n_groups), SUB * ((t - edge) // n_groups) + SUB)
                e_tile, w_tile, q = r_e[p, rows], r_w[p, rows], (t - edge) % n_groups
            else:
                e_tile, w_tile, q = r_ne[p], r_nw[p], t - (H + ny) // SUB
            e_tile = turn(e_tile, -H * q) if q else e_tile
            w_tile = turn(w_tile, H * (n_groups - 1 - q)) if q != n_groups - 1 else w_tile
            side = jnp.where(group == 0, e_tile, jnp.where(group == n_groups - 1, w_tile, 0.0))
            ext[p, SUB * t:SUB * t + SUB, nx:] = side

    for c in planes:
        c.wait()
    kmt = kmt_v[...].astype(F32)
    ext[(KMT, *own)] = kmt
    for p in range(FX):
        pack(p)
    pl.semaphore_wait(barrier, len(where_to))
    first = wide_copies(KMT, FX)

    dz = ext[(DEPTH, *own)] / jnp.maximum(kmt, 1.0)
    safe = jnp.where(kmt > 0, dz, 1.0)
    zero = jnp.zeros((ny, nx), F32)
    wet_v[...] = kmt
    dz_v[...] = dz
    cc_v[...] = (TIME_STEP * DIFF_KT) / (safe * safe)
    cum_v[...] = zero
    for ref in (tb, sb, pu, pv):
        ref[0] = zero
        ref[n_lev + 1] = zero
    for ref in (gc, gu, gv):
        ref[0] = zero + 1.0
    for ref in (bank_uv, bank_ts, sc_w, su_e):
        ref[...] = jnp.zeros(ref.shape, F32)
    lane = iota((ny, LANES), 1)
    even = lane % 2 == 0

    def both_edges(x):
        return jnp.where(lane < LANES // 2, x[:, :LANES], x[:, nx - LANES:])

    def down_levels(k0):
        g, t_up, s_up, cum = gc[k0], tb[k0], sb[k0], cum_v[...]
        wet = k0.astype(F32) < wet_v[...]
        for d in range(UN):
            k = k0 + d
            below = (k + 1).astype(F32) < wet_v[...]
            t, s = tb[k + 1], sb[k + 1]
            dens = jnp.where(wet, BETA_S * (s - 1.0) - ALPHA_T * (t - 1.0), 0.0)
            cum = cum + dens
            pres = dz_v[...] * (cum - 0.5 * dens)
            pp[k] = pres
            coef = cc_v[...]
            up = jnp.where(below, coef, 0.0)
            inv = reduced(1.0 + up + coef * (1.0 - g))
            g = up * inv
            t_up = jnp.where(wet, (t + coef * t_up) * inv, 0.0)
            s_up = jnp.where(wet, (s + coef * s_up) * inv, 0.0)
            gc[k + 1] = g
            tb[k + 1] = t_up
            sb[k + 1] = s_up
            wet = below
            u, v = ub[k], vb[k]
            b, m = slot_of(k, bank)
            here = ((lane + 1 - m) & LAST) < 2
            pltpu.store(bank_uv.at[0, b], turn(both_edges(u), m), mask=here)
            pltpu.store(bank_uv.at[1, b], turn(both_edges(v), m), mask=here)
            pltpu.store(sc_w.at[2], turn(pres[:, :LANES], m + b), mask=lane == m + b)
            sr_s[k, FIRST] = u[first_row]
            sr_s[k, SECOND] = v[first_row]
            sp_s[k] = pres[first_row]
            sr_n[k, FIRST] = u[last_row]
            sr_n[k, SECOND] = v[last_row]
        cum_v[...] = cum

    def down_chunk(c, carry):
        for a in range(4):
            load(a, c).wait()

        def levels(i, carry):
            down_levels(c * CH + i * UN)
            return carry

        return lax.fori_loop(0, CH // UN, levels, carry)

    lax.fori_loop(0, n_chunk, down_chunk, 0)

    def split_banks(banks):
        a, b = banks[0], turn(banks[1], 1)
        return jnp.where(even, a, b), turn(jnp.where(even, b, a), 1)

    for i in range(2):
        sc_w[i], sc_e[i] = split_banks(bank_uv.at[i])
    second = started([
        remote(sc_w, rc_e, "w"),
        remote(sc_e, rc_w, "e"),
        remote(sr_n, rr_s, "n"),
        remote(sr_s, rr_n, "s"),
        remote(sp_s, rp_n, "s"),
        remote(sc_e.at[0, pl.ds(0, SUB)], rc_nw, "se"),
        remote(sc_w.at[1, pl.ds(ny - SUB, SUB)], rc_se, "nw"),
    ])

    def store_out(a, c):
        src, dst = ((tb, tm_out), (sb, sm_out), (pu, us_out), (pv, vs_out))[a]
        return pltpu.make_async_copy(src.at[pl.ds(c * CH + 1, CH)], dst.at[pl.ds(c * CH, CH)], out_sem.at[a, c])

    def upward(a, level):
        def chunk(j, carry):
            c = n_chunk - 1 - j

            def levels(i, carry):
                level(c * CH + CH - 1 - i * UN)
                return carry

            lax.fori_loop(0, CH // UN, levels, 0)
            store_out(a, c).start()
            store_out(a + 1, c).start()
            return carry

        lax.fori_loop(0, n_chunk, chunk, 0)

    def mix_levels(k0):
        t, s = tb[k0 + 2], sb[k0 + 2]
        for d in range(UN):
            k = k0 - d
            g = gc[k + 1]
            t = tb[k + 1] + g * t
            s = sb[k + 1] + g * s
            tb[k + 1] = t
            sb[k + 1] = s
            b, m = slot_of(k, bank)
            here = ((lane + 1 - m) & LAST) < 2
            pltpu.store(bank_ts.at[0, b], turn(both_edges(t), m), mask=here)
            pltpu.store(bank_ts.at[1, b], turn(both_edges(s), m), mask=here)
            tr_s[k, FIRST] = t[first_row]
            tr_s[k, SECOND] = s[first_row]
            tr_n[k, FIRST] = t[last_row]
            tr_n[k, SECOND] = s[last_row]

    upward(0, mix_levels)
    for i in range(2):
        tc_w[i], tc_e[i] = split_banks(bank_ts.at[i])

    for c in first:
        c.wait()
    for p in range(FX):
        unpack(p)
    line = iota((whole, wide), 0)
    seen = ((line >= H) | (row > 0)) & ((line < H + ny) | (row < n_rows - 1))
    kx = jnp.where(seen, ext[KMT], 0.0)
    ext[KMT] = kx
    dzx = ext[DEPTH] / jnp.maximum(kx, 1.0)
    ku = jnp.minimum(kx, pltpu.roll(kx, wide - 1, 1))
    kv = jnp.minimum(kx, pltpu.roll(kx, whole - 1, 0))
    dzu = 0.5 * (dzx + pltpu.roll(dzx, wide - 1, 1))
    dzv = 0.5 * (dzx + pltpu.roll(dzx, whole - 1, 0))
    xp[KU] = ku
    xp[KV] = kv
    xp[DZU] = dzu
    xp[DZV] = dzv
    xp[GU] = jnp.where(ku > 0, dt_sub * (ku * dzu), 0.0)
    xp[GV] = jnp.where(kv > 0, dt_sub * (kv * dzv), 0.0)
    xp[WD] = jnp.where(kx > 0, dt_sub, 0.0)
    ext[ETA] = jnp.where(kx > 0, ext[ETA], 0.0)
    ext[TU] = jnp.where(ku > 0, ext[TU], 0.0)
    ext[TV] = jnp.where(kv > 0, ext[TV], 0.0)
    face_out[2] = wet_v[...]
    for i in range(2):
        count = xp[(KU + i, *own)]
        safe = jnp.where(count > 0, xp[(DZU + i, *own)], 1.0)
        faces[i] = count
        face_out[i] = count
        coefs[i] = (TIME_STEP * VISC_KV) / (safe * safe)
        push_v[i] = zero
        sum_v[i] = zero

    for c in second:
        c.wait_recv()
    pair = lane // 2
    lev = jnp.where(pair < bank, pair + bank * (lane % 2), n_lev).astype(F32)

    def column(ref, count):
        return jnp.where(lev < count, ref, 0.0)

    u_w = column(rc_w[0], xp[KU, mid, at_w])
    v_w = column(rc_w[1], xp[KV, mid, at_w])
    u_e = column(rc_e[0], xp[KU, mid, at_e])
    v_e = column(rc_e[1], xp[KV, mid, at_e])
    u_last = column(sc_e[0], xp[KU, mid, nx - 1:nx])
    v_zero = column(sc_w[1], xp[KV, mid, FIRST])
    corner_u = jnp.where(lev[FIRST] < xp[KU, at_n, at_w], rc_nw[FIRST, :], 0.0)
    q_e = 0.25 * (u_last + u_e) * (u_last + u_e) + rc_e[2]
    c_w = (u_w + shift_north(u_w, corner_u)) * (v_w + v_zero)
    hc[0, 0], hc[0, 1] = merged(u_w, q_e)
    hc[1, 0], hc[1, 1] = merged(c_w, v_e)
    corner_p[...] = jnp.where(lev[:SUB] < xp[KV, H - SUB:H, at_e], rc_se[...], 0.0)

    def momentum_levels(i, carry):
        k0 = i * UM
        parts = [pu[k0], pv[k0]]
        gains = [gu[k0], gv[k0]]
        wets = [k0.astype(F32) < faces[f] for f in range(2)]
        for d in range(UM):
            k = k0 + d
            kf = k.astype(F32)
            u = jnp.where(wets[0], ub[k], 0.0)
            v = jnp.where(wets[1], vb[k], 0.0)
            p = pp[k]
            b, m = slot_of(k, bank)
            edge_uq = turn(hc[0, b], LANES - m)
            edge_cv = turn(hc[1, b], LANES - m)
            rows_n, rows_s = rr_n[k], rr_s[k]
            u_n = jnp.where(kf < xp[KU, at_n, cols], rows_n[FIRST], 0.0)
            v_n = jnp.where(kf < xp[KV, at_n, cols], rows_n[SECOND], 0.0)
            u_s = jnp.where(kf < xp[KU, at_s, cols], rows_s[FIRST], 0.0)
            v_s = jnp.where(kf < xp[KV, at_s, cols], rows_s[SECOND], 0.0)
            corner_v = turn(corner_p[...], LAST - m - b)[SUB - 1:]
            v_s8 = jnp.broadcast_to(v_s, (SUB, nx))
            v_s_e = shift_east(v_s8, jnp.broadcast_to(corner_v, (SUB, LANES)))[FIRST]

            cen_u = shift_west(u, edge_uq) + u
            head_u = 0.25 * (cen_u * cen_u) + p
            corner = (u + shift_north(u, u_n)) * (v + shift_east(v, edge_cv))
            corner_s = (u_s + u[first_row]) * (v_s + v_s_e)
            grad_u = (shift_east(head_u, edge_uq) - head_u) + 0.25 * (corner - shift_south(corner, corner_s))
            cen_v = shift_south(v, v_s) + v
            head_v = 0.25 * (cen_v * cen_v) + p
            edge_v = v[last_row] + v_n
            edge_v = 0.25 * (edge_v * edge_v) + rp_n[k]
            grad_v = (shift_north(head_v, edge_v) - head_v) + 0.25 * (corner - shift_west(corner, edge_cv))
            for f, grad, now, part, gain in ((0, grad_u, u, pu, gu), (1, grad_v, v, pv, gv)):
                below = kf + 1.0 < faces[f]
                push = jnp.where(wets[f], -TIME_STEP * grad, 0.0)
                source = now + push
                push_v[f] += push
                sum_v[f] += source
                coef = coefs[f]
                up = jnp.where(below, coef, 0.0)
                inv = reduced(1.0 + up + coef * (1.0 - gains[f]))
                gains[f] = up * inv
                parts[f] = jnp.where(wets[f], (source + coef * parts[f]) * inv, 0.0)
                gain[k + 1] = gains[f]
                part[k + 1] = parts[f]
                wets[f] = below
        return carry

    lax.fori_loop(0, n_lev // UM, momentum_levels, 0)

    for f in range(2):
        ext[(FX + f, *own)] = xp[(DZU + f, *own)] * push_v[f] * (1.0 / TIME_STEP)
        pack(FX + f)
    third = wide_copies(FX, 2)
    tracer = started([
        remote(tc_w, qc_e, "w"),
        remote(tc_e, qc_w, "e"),
        remote(tr_n, qr_s, "n"),
        remote(tr_s, qr_n, "s"),
    ])

    def rise_levels(k0):
        u, v = pu[k0 + 2], pv[k0 + 2]
        for d in range(UN):
            k = k0 - d
            u = pu[k + 1] + gu[k + 1] * u
            v = pv[k + 1] + gv[k + 1] * v
            pu[k + 1] = u
            pv[k + 1] = v
            b, m = slot_of(k, bank)
            pltpu.store(su_e, turn(u[:, nx - LANES:], m + b + 1), mask=lane == m + b)
            sv_n[k] = v[last_row]

    upward(2, rise_levels)
    fourth = started([remote(su_e, ru_w, "e"), remote(sv_n, rv_s, "n")])

    for c in third:
        c.wait_recv()
    for f in range(2):
        unpack(FX + f)
        xp[BU + f] = jnp.where(xp[KU + f] > 0, dt_sub * ext[FX + f], 0.0)
    acc[...] = jnp.zeros(acc.shape, F32)
    norm = 6.0 / (n_sub * (n_sub + 1) * (n_sub + 2))
    tiles = whole // SUB
    line8 = iota((SUB, wide), 0)
    t0 = H // SUB - 1

    def substep(n, carry):
        tide_u, tide_v = tide[n, 0], tide[n, 1]
        weight = norm * ((n + 1) * (n_sub - n)).astype(F32)

        def finish(t, eta, rolled, rolled_next, u, v):
            rows = slice(SUB * t, SUB * t + SUB)
            eta_n = jnp.where(line8 == SUB - 1, rolled_next, rolled)
            eta_e = pltpu.roll(eta, wide - 1, 1)
            u_new = u + (xp[GU, rows] * (tide_u + (eta - eta_e)) + xp[BU, rows])
            v_new = v + (xp[GV, rows] * (tide_v + (eta - eta_n)) + xp[BV, rows])
            ext[TU, rows] = u_new
            ext[TV, rows] = v_new
            if t0 <= t < (H + ny) // SUB:
                at = slice(SUB * (t - t0), SUB * (t - t0) + SUB)
                acc[0, at] += weight * u_new
                acc[1, at, :nx] += weight * v_new[:, :nx]

        last = None
        v_below = jnp.zeros((SUB, wide), F32)
        for t in range(tiles):
            rows = slice(SUB * t, SUB * t + SUB)
            u, v = ext[TU, rows], ext[TV, rows]
            v_roll = pltpu.roll(v, 1, 0)
            v_s = jnp.where(line8 == 0, v_below, v_roll)
            v_below = v_roll
            eta = ext[ETA, rows] - xp[WD, rows] * ((u - pltpu.roll(u, 1, 1)) + (v - v_s))
            ext[ETA, rows] = eta
            rolled = pltpu.roll(eta, SUB - 1, 0)
            if last is not None:
                eta_b, rolled_b, u_b, v_b = last
                finish(t - 1, eta_b, rolled_b, rolled, u_b, v_b)
            last = (eta, rolled, u, v)
        finish(tiles - 1, eta, rolled, rolled, u, v)
        return carry

    lax.fori_loop(0, n_sub, substep, 0)
    for i in range(3):
        bar_out[i] = ext[(ETA + i, *own)]

    def safe_depth(f, rows, lanes):
        depth = xp[KU + f, rows, lanes] * xp[DZU + f, rows, lanes]
        return jnp.where(depth > 0, depth, 1.0)

    inner = slice(SUB, SUB + ny)
    for f in range(2):
        corr_out[f] = (acc[f, inner, cols] - xp[DZU + f, mid, cols] * sum_v[f]) / safe_depth(f, mid, cols)
    for c in fourth:
        c.wait_recv()
    star = ru_w[...]
    fix = (acc[0, inner, at_w] - xp[DZU, mid, at_w] * jnp.sum(star, axis=1, keepdims=True)) / safe_depth(0, mid, at_w)
    u_c = column(star + fix, xp[KU, mid, at_w])
    star = rv_s[...]
    fix = (acc[1, SUB - 1:SUB, cols] - xp[DZV, at_s, cols] * jnp.sum(star, axis=0)) / safe_depth(1, at_s, cols)
    levels = iota(star.shape, 0).astype(F32)
    vcs_out[...] = jnp.where(levels < xp[KV, at_s, cols][None], star + fix[None], 0.0)
    for c in tracer:
        c.wait_recv()
    for i in range(2):
        halo_out[i, 0], halo_out[i, 1] = merged(u_c * (qc_w[i] + tc_w[i]), qc_e[i])
    trow_n_out[...] = qr_n[...]
    trow_s_out[...] = qr_s[...]
    for c in second + third + tracer + fourth:
        c.wait_send()
    for c in range(n_chunk):
        for a in range(4):
            store_out(a, c).wait()


def last_kernel(us, vs, tm, sm, bar, corr, faces, vcs, halo, trow_n, trow_s,
                eta_out, tu_out, tv_out, u_out, v_out, t_out, s_out, *, bank):
    step = pl.program_id(0)

    @pl.when(step == 0)
    def _():
        for i, ref in enumerate((eta_out, tu_out, tv_out)):
            ref[...] = bar[i]

    for i in range(KB):
        k = step * KB + i
        kf = k.astype(F32)
        u = jnp.where(kf < faces[0], us[i] + corr[0], 0.0)
        v = jnp.where(kf < faces[1], vs[i] + corr[1], 0.0)
        u_out[i] = u
        v_out[i] = v
        wet = kf < faces[2]
        v_s = vcs[k]
        rows_n, rows_s = trow_n[k], trow_s[k]
        b, m = slot_of(k, bank)
        for a, src, dst in ((0, tm, t_out), (1, sm, s_out)):
            x = src[i]
            edge = turn(halo[a, b], LANES - m)
            flux_x = u * (x + shift_east(x, edge))
            flux_y = v * (x + shift_north(x, rows_n[a:a + 1]))
            edge_y = v_s * (rows_s[a:a + 1] + x[FIRST])
            div = flux_x - shift_west(flux_x, edge) + flux_y - shift_south(flux_y, edge_y)
            dst[i] = jnp.where(wet, x - (0.5 * TIME_STEP) * div, 0.0)


def solution(mesh):
    n_cols, n_rows = mesh.shape["col"], mesh.shape["row"]

    def local_step(vel_u, vel_v, value_a11, salinity, sea_level, trans_u, trans_v, bathymetry, kmt_levels, tide_force):
        n_lev, ny, nx = vel_u.shape
        whole, wide = ny + 2 * H, nx + LANES
        n_chunk, bank = n_lev // CH, (n_lev + 1) // 2
        any_spec = pl.BlockSpec(memory_space=pl.ANY)
        vmem_spec = pl.BlockSpec(memory_space=pltpu.VMEM)
        cube = (n_lev, ny, nx)
        deep = (n_lev + 2, ny, nx)
        column, pair_c, rows1, rows2 = (ny, LANES), (2, ny, LANES), (n_lev, 1, nx), (n_lev, 2, nx)
        banks, two, small = (2, 2, ny, LANES), (2, ny, nx), (SUB, LANES)

        def sds(*shape):
            return jax.ShapeDtypeStruct(shape, F32)

        def bufs(*shapes):
            return [pltpu.VMEM(shape, F32) for shape in shapes]

        def sems(*shape):
            return pltpu.SemaphoreType.DMA(shape)

        passed = [(3, ny, nx), two, (3, ny, nx), rows1, banks, rows2, rows2]
        *cubes, bar, corr, face, vcs, halo, trow_n, trow_s = pl.pallas_call(
            functools.partial(main_kernel, n_rows, n_cols),
            out_shape=[sds(*s) for s in [cube] * 4 + passed],
            in_specs=[any_spec] * 9 + [pl.BlockSpec(memory_space=pltpu.SMEM)],
            out_specs=[any_spec] * 4 + [vmem_spec] * len(passed),
            scratch_shapes=[
                pltpu.VMEM((ny, nx), jnp.int32),
                *bufs((7, whole, wide), (9, whole, wide), (2, ny + SUB, wide)),
                *bufs(*[(7, 3 * SUB, LANES)] * 2, *[(7, 2 * SUB, LANES)] * 2, *[(7, SUB, LANES)] * 4),
                *bufs(cube, cube, *[deep] * 7, cube, *[(ny, nx)] * 4, two, two, two, two),
                *bufs(banks, banks, (3, ny, LANES), pair_c, (3, ny, LANES), pair_c, small, small, banks, small),
                *bufs(rows2, rows2, rows1, rows2, rows2, rows1),
                *bufs(pair_c, pair_c, rows2, rows2, pair_c, pair_c, rows2, rows2, column, rows1, column, rows1),
                sems(5), sems(4, n_chunk), sems(4, n_chunk), sems(29), sems(29),
            ],
            compiler_params=pltpu.CompilerParams(collective_id=0, has_side_effects=True, vmem_limit_bytes=56 * 2**20),
        )(kmt_levels, bathymetry, sea_level, trans_u, trans_v, vel_u, vel_v, value_a11, salinity, tide_force)

        block = pl.BlockSpec((KB, ny, nx), lambda i: (i, 0, 0))

        def full(*shape):
            return pl.BlockSpec(shape, lambda i: (0,) * len(shape))

        return pl.pallas_call(
            functools.partial(last_kernel, bank=bank),
            grid=(n_lev // KB,),
            out_shape=[sds(ny, nx)] * 3 + [sds(*cube)] * 4,
            in_specs=[block] * 4 + [full(*s) for s in passed],
            out_specs=[full(ny, nx)] * 3 + [block] * 4,
        )(*cubes, bar, corr, face, vcs, halo, trow_n, trow_s)

    spec_cube = P(None, "row", "col")
    spec_plane = P("row", "col")
    return jax.shard_map(local_step, mesh=mesh, in_specs=(spec_cube,) * 4 + (spec_plane,) * 5 + (P(None, None),),
                         out_specs=(spec_plane,) * 3 + (spec_cube,) * 4, check_vma=False)
```

profile of v0, /device:TPU:0, one launch (start us, length us, event | category | flops | bytes accessed | tf_op | source)
XLA Modules:
  0.0 68.6 jit_solution(12112302803763344648)
XLA Ops:
  0.6 1.4 %copy.17.tide = f32[30,2]{1,0:T(8,128)} copy(f32[30,2]{0,1:T(2,128)} %param.19) | data formatting | bytes 480 | tf_op args[9]
  2.0 46.6 %shard_map.153 = (f32[75,48,256]{2,1,0:T(8,128)}, f32[75,48,256]{2,1,0:T(8,128)}, f32[75,48,256]{2,1,0:T(8,128)}, f32[75,48,256]{2,1,0:T(8,128)}, f32[3,48,256]{...) custom-call(s32[48,256]{1,0:T(8,128)} %kmt_in.1, ...), custom_call_target="tpu_custom_call" | custom-call | tf_op jit(solution)/shard_map/pallas_call | solution.py:585
  48.7 19.9 %shard_map.154 = (f32[48,256]{1,0:T(8,128)}, f32[48,256]{1,0:T(8,128)}, f32[48,256]{1,0:T(8,128)}, f32[75,48,256]{2,1,0:T(8,128)}, f32[75,48,256]{2,1,0:T(8,128)...) custom-call(f32[75,48,256]{2,1,0:T(8,128)} %get-tuple-element.18.us, f32[75,48,256]{2,1,0:T(8,128)} %get-tuple-element.19.vs, ...), custom_call_target="tpu_custom_call" | custom-call | tf_op jit(solution)/shard_map/pallas_call | solution.py:608
where the time goes:
time: 69.2 us; the launch traced here: 68.6 us
  Pallas kernels  66.6 us (96%)
  local copies, waits for them, and re-layouts  1.37 us (2%)
    pallas_call x1, Pallas kernels, local_step(): pl.pallas_call(functools.partial(main_kernel, n_rows, n_cols), out_shape=...  46.6 us
    pallas_call x1, Pallas kernels, local_step(): pl.pallas_call(functools.partial(last_kernel, bank=bank), grid=(n_lev //...  19.9 us

commit v1 on v0

v1 whole, which is shorter than its diff:
```python
import functools

import jax
import jax.numpy as jnp
from jax import lax
from jax.experimental import pallas as pl
from jax.experimental.pallas import tpu as pltpu
from jax.sharding import PartitionSpec as P

TIME_STEP = 4.0
ALPHA_T = 0.02
BETA_S = 0.015
VISC_KV = 0.001
DIFF_KT = 0.0005
MESH = pl.DeviceIdType.MESH
H = 32
CH = 15
UN = 5
UE = 15
KB = 5
SUB, LANES = 8, 128
LAST = LANES - 1
F32 = jnp.float32
HEAD = 0.25 * TIME_STEP
KMT, DEPTH, ETA, TU, TV, FX, FY = range(7)
KU, KV, DZU, DZV, GU, GV, BU, BV, WD, GW, BW, UW = range(12)
FIRST, SECOND = slice(0, 1), slice(1, 2)


def iota(shape, axis):
    return lax.broadcasted_iota(jnp.int32, shape, axis)


def reduced(x):
    return pl.reciprocal(x, approx=False)


def scaled(x):
    return x if HEAD == 1.0 else HEAD * x


def lane_of(x):
    return iota(x.shape, 1)


def slot_of(k, bank):
    b = (k >= bank).astype(jnp.int32)
    return b, 2 * (k - b * bank)


def turn(x, n):
    return pltpu.roll(x, n % LANES if isinstance(n, int) else n, 1)


def shift_east(x, halo):
    left, right = turn(x[:, :LANES], -1), turn(x[:, LANES:], -1)
    edge = lane_of(left) == LAST
    return jnp.concatenate([jnp.where(edge, right, left), jnp.where(edge, halo, right)], axis=1)


def shift_west(x, halo):
    left, right = turn(x[:, :LANES], 1), turn(x[:, LANES:], 1)
    edge = lane_of(left) == 0
    return jnp.concatenate([jnp.where(edge, halo, left), jnp.where(edge, left, right)], axis=1)


def tiles_of(x):
    return [x[SUB * t:SUB * t + SUB] for t in range(x.shape[0] // SUB)]


def shift_north(x, halo):
    rolled = [pltpu.roll(t, SUB - 1, 0) for t in tiles_of(x)]
    edge = iota(rolled[0].shape, 0) == SUB - 1
    rolled.append(jnp.broadcast_to(halo, rolled[0].shape))
    return jnp.concatenate([jnp.where(edge, b, a) for a, b in zip(rolled[:-1], rolled[1:])], axis=0)


def shift_south(x, halo):
    rolled = [pltpu.roll(t, 1, 0) for t in tiles_of(x)]
    edge = iota(rolled[0].shape, 0) == 0
    rolled.insert(0, jnp.broadcast_to(halo, rolled[0].shape))
    return jnp.concatenate([jnp.where(edge, a, b) for a, b in zip(rolled[:-1], rolled[1:])], axis=0)


def merged(west, east):
    even = lane_of(west) % 2 == 0
    back = turn(east, -1)
    return jnp.where(even, west, back), turn(jnp.where(even, back, west), -1)


def main_kernel(n_rows, n_cols,
                kmt_in, bat_in, eta_in, tu_in, tv_in, u_in, v_in, t_in, s_in, tide,
                pu, pv, tb, sb, bar_out, corr_out, face_out, vcs_out,
                halo_out, trow_n_out, trow_s_out,
                kmt_v, ext, xp, acc, pk_w, pk_e, r_e, r_w, r_ne, r_nw, r_se, r_sw,
                ub, vb, gc, gu, gv, pp, wet_v, dz_v, cc_v, cum_v, faces, coefs, push_v, sum_v, s_now, s_head, s_corner, s_side, s_edge,
                bank_uv, bank_ts, sc_w, sc_e, sp_w, rc_e, rc_w, rp_e, rc_nw, rc_se, hc, corner_p,
                sr_n, sr_s, sp_s, rr_n, rr_s, rp_n,
                tc_w, tc_e, tr_n, tr_s, qc_e, qc_w, qr_n, qr_s, su_e, sv_n, ru_w, rv_s,
                plane_sem, in_sem, send_sem, recv_sem):
    n_sub = tide.shape[1]
    n_lev = u_in.shape[0]
    n_chunk = n_lev // CH
    bank = (n_lev + 1) // 2
    ny, nx = kmt_in.shape
    dt_sub = TIME_STEP / n_sub
    col, row = lax.axis_index("col"), lax.axis_index("row")
    east, west = lax.rem(col + 1, n_cols), lax.rem(col + n_cols - 1, n_cols)
    north, south = lax.rem(row + 1, n_rows), lax.rem(row + n_rows - 1, n_rows)
    where_to = {"n": (col, north), "s": (col, south), "e": (east, row), "w": (west, row),
                "ne": (east, north), "nw": (west, north), "se": (east, south), "sw": (west, south)}
    own = (pl.ds(H, ny), pl.ds(0, nx))
    mid, cols = slice(H, H + ny), slice(0, nx)
    at_n, at_s = slice(H + ny, H + ny + 1), slice(H - 1, H)
    whole, wide = ny + 2 * H, nx + LANES
    at_w, at_e = slice(wide - 1, wide), slice(nx, nx + 1)
    first_row, last_row = FIRST, slice(ny - 1, ny)

    planes = [pltpu.make_async_copy(kmt_in, kmt_v, plane_sem.at[KMT])]
    for i, ref in ((DEPTH, bat_in), (ETA, eta_in), (TU, tu_in), (TV, tv_in)):
        planes.append(pltpu.make_async_copy(ref, ext.at[(i, *own)], plane_sem.at[i]))
    for c in planes:
        c.start()

    def load(a, c):
        src, dst, off = ((u_in, ub, 0), (v_in, vb, 0), (t_in, tb, 1), (s_in, sb, 1))[a]
        return pltpu.make_async_copy(src.at[pl.ds(c * CH, CH)], dst.at[pl.ds(c * CH + off, CH)], in_sem.at[a, c])

    for a in (0, 2):
        for c in range(n_chunk):
            load(a, c).start()
            load(a + 1, c).start()

    barrier = pltpu.get_barrier_semaphore()
    for c_id, r_id in where_to.values():
        pl.semaphore_signal(barrier, inc=1, device_id={"col": c_id, "row": r_id}, device_id_type=MESH)

    used = []

    def remote(src, dst, to):
        c_id, r_id = where_to[to]
        i = len(used)
        used.append(i)
        return pltpu.make_async_remote_copy(src_ref=src, dst_ref=dst, send_sem=send_sem.at[i], recv_sem=recv_sem.at[i],
                                            device_id={"col": c_id, "row": r_id}, device_id_type=MESH)

    def started(copies):
        for c in copies:
            c.start()
        return copies

    def wide_copies(p0, n):
        ps = pl.ds(p0, n)
        low, mids, high = pl.ds(0, 2 * SUB), pl.ds(0, SUB), pl.ds(2 * SUB, SUB)
        return started([
            remote(ext.at[ps, pl.ds(H, H), pl.ds(0, nx)], ext.at[ps, pl.ds(H + ny, H), pl.ds(0, nx)], "s"),
            remote(ext.at[ps, pl.ds(ny, H), pl.ds(0, nx)], ext.at[ps, pl.ds(0, H), pl.ds(0, nx)], "n"),
            remote(pk_w.at[ps, low], r_e.at[ps], "w"),
            remote(pk_e.at[ps, low], r_w.at[ps], "e"),
            remote(pk_w.at[ps, mids], r_ne.at[ps], "sw"),
            remote(pk_e.at[ps, mids], r_nw.at[ps], "se"),
            remote(pk_w.at[ps, high], r_se.at[ps], "nw"),
            remote(pk_e.at[ps, high], r_sw.at[ps], "ne"),
        ])

    group = iota((SUB, LANES), 1) // H
    n_groups = LANES // H

    def pack(p):
        x = ext[(p, *own)]
        for ref, tile, g0 in ((pk_w, x[:, :LANES], 0), (pk_e, x[:, nx - LANES:], n_groups - 1)):
            for at, first, count in ((0, 0, 4), (1, 4, 2), (2, 2, 4)):
                total = jnp.zeros((SUB, LANES), F32)
                for q in range(count):
                    rows = tile[SUB * (first + q):SUB * (first + q) + SUB]
                    rows = turn(rows, H * (q - g0)) if q != g0 else rows
                    total = jnp.where(group == q, rows, total)
                ref[p, SUB * at:SUB * at + SUB, :] = total

    def unpack(p):
        edge = H // SUB
        for t in range(whole // SUB):
            if t < edge:
                e_tile, w_tile, q = r_se[p], r_sw[p], t
            elif t < (H + ny) // SUB:
                rows = slice(SUB * ((t - edge) // n_groups), SUB * ((t - edge) // n_groups) + SUB)
                e_tile, w_tile, q = r_e[p, rows], r_w[p, rows], (t - edge) % n_groups
            else:
                e_tile, w_tile, q = r_ne[p], r_nw[p], t - (H + ny) // SUB
            e_tile = turn(e_tile, -H * q) if q else e_tile
            w_tile = turn(w_tile, H * (n_groups - 1 - q)) if q != n_groups - 1 else w_tile
            side = jnp.where(group == 0, e_tile, jnp.where(group == n_groups - 1, w_tile, 0.0))
            ext[p, SUB * t:SUB * t + SUB, nx:] = side

    for c in planes:
        c.wait()
    kmt = kmt_v[...].astype(F32)
    ext[(KMT, *own)] = kmt
    for p in range(FX):
        pack(p)
    pl.semaphore_wait(barrier, len(where_to))
    first = wide_copies(KMT, FX)

    zero = jnp.zeros((ny, nx), F32)
    for ref in (bank_uv, bank_ts, sp_w, su_e):
        ref[...] = jnp.zeros(ref.shape, F32)
    lane = iota((ny, LANES), 1)
    even = lane % 2 == 0

    def both_edges(x):
        return jnp.where(lane < LANES // 2, x[:, :LANES], x[:, nx - LANES:])

    def gather(x, y, k, banks, rows_s, rows_n):
        b, m = slot_of(k, bank)
        here = ((lane + 1 - m) & LAST) < 2
        pltpu.store(banks.at[0, b], turn(both_edges(x), m), mask=here)
        pltpu.store(banks.at[1, b], turn(both_edges(y), m), mask=here)
        rows_s[k, FIRST] = x[first_row]
        rows_s[k, SECOND] = y[first_row]
        rows_n[k, FIRST] = x[last_row]
        rows_n[k, SECOND] = y[last_row]

    def in_chunks(arrays, levels, step):
        def chunk(c, carry):
            for a in arrays:
                load(a, c).wait()

            def group_of(i, carry):
                levels(c * CH + i * step)
                return carry

            return lax.fori_loop(0, CH // step, group_of, carry)

        lax.fori_loop(0, n_chunk, chunk, 0)

    def edge_levels(k0):
        for d in range(UE):
            gather(ub[k0 + d], vb[k0 + d], k0 + d, bank_uv, sr_s, sr_n)

    in_chunks((0, 1), edge_levels, UE)

    def split_banks(banks):
        a, b = banks[0], turn(banks[1], 1)
        return jnp.where(even, a, b), turn(jnp.where(even, b, a), 1)

    for i in range(2):
        sc_w[i], sc_e[i] = split_banks(bank_uv.at[i])
    second = started([
        remote(sc_w, rc_e, "w"),
        remote(sc_e, rc_w, "e"),
        remote(sr_n, rr_s, "n"),
        remote(sr_s, rr_n, "s"),
        remote(sc_e.at[0, pl.ds(0, SUB)], rc_nw, "se"),
        remote(sc_w.at[1, pl.ds(ny - SUB, SUB)], rc_se, "nw"),
    ])

    dz = ext[(DEPTH, *own)] / jnp.maximum(kmt, 1.0)
    safe = jnp.where(kmt > 0, dz, 1.0)
    wet_v[...] = kmt
    dz_v[...] = TIME_STEP * dz
    cc_v[...] = (TIME_STEP * DIFF_KT) / (safe * safe)
    cum_v[...] = zero
    for ref in (tb, sb, pu, pv):
        ref[0] = zero
        ref[n_lev + 1] = zero
    for ref in (gc, gu, gv):
        ref[0] = zero + 1.0

    def pressure_levels(k0):
        cum = cum_v[...]
        for d in range(UE):
            k = k0 + d
            dens = BETA_S * (sb[k + 1] - 1.0) - ALPHA_T * (tb[k + 1] - 1.0)
            dens = jnp.where(k.astype(F32) < wet_v[...], dens, 0.0)
            cum = cum + dens
            pres = dz_v[...] * (cum - 0.5 * dens)
            pp[k] = pres
            b, m = slot_of(k, bank)
            pltpu.store(sp_w, turn(pres[:, :LANES], m + b), mask=lane == m + b)
            sp_s[k] = pres[first_row]
        cum_v[...] = cum

    in_chunks((2, 3), pressure_levels, UE)
    second += started([remote(sp_w, rp_e, "w"), remote(sp_s, rp_n, "s")])

    def down_levels(i, carry):
        k0 = i * UN
        g, t_up, s_up = gc[k0], tb[k0], sb[k0]
        wet = k0.astype(F32) < wet_v[...]
        for d in range(UN):
            k = k0 + d
            below = (k + 1).astype(F32) < wet_v[...]
            coef = cc_v[...]
            up = jnp.where(below, coef, 0.0)
            inv = reduced(1.0 + up + coef * (1.0 - g))
            g = up * inv
            t_up = jnp.where(wet, (tb[k + 1] + coef * t_up) * inv, 0.0)
            s_up = jnp.where(wet, (sb[k + 1] + coef * s_up) * inv, 0.0)
            gc[k + 1] = g
            tb[k + 1] = t_up
            sb[k + 1] = s_up
            wet = below
        return carry

    lax.fori_loop(0, n_lev // UN, down_levels, 0)

    for c in first:
        c.wait()
    for p in range(FX):
        unpack(p)
    line = iota((whole, wide), 0)
    seen = ((line >= H) | (row > 0)) & ((line < H + ny) | (row < n_rows - 1))
    kx = jnp.where(seen, ext[KMT], 0.0)
    ext[KMT] = kx
    dzx = ext[DEPTH] / jnp.maximum(kx, 1.0)
    ku = jnp.minimum(kx, pltpu.roll(kx, wide - 1, 1))
    kv = jnp.minimum(kx, pltpu.roll(kx, whole - 1, 0))
    dzu = 0.5 * (dzx + pltpu.roll(dzx, wide - 1, 1))
    dzv = 0.5 * (dzx + pltpu.roll(dzx, whole - 1, 0))
    xp[KU] = ku
    xp[KV] = kv
    xp[DZU] = dzu
    xp[DZV] = dzv
    xp[GU] = jnp.where(ku > 0, dt_sub * (ku * dzu), 0.0)
    xp[GV] = jnp.where(kv > 0, dt_sub * (kv * dzv), 0.0)
    xp[WD] = jnp.where(kx > 0, dt_sub, 0.0)
    xp[GW] = pltpu.roll(xp[GU], 1, 1)
    ext[ETA] = jnp.where(kx > 0, ext[ETA], 0.0)
    ext[TU] = jnp.where(ku > 0, ext[TU], 0.0)
    ext[TV] = jnp.where(kv > 0, ext[TV], 0.0)
    xp[UW] = pltpu.roll(ext[TU], 1, 1)
    face_out[2] = wet_v[...]
    for i in range(2):
        count = xp[(KU + i, *own)]
        safe = jnp.where(count > 0, xp[(DZU + i, *own)], 1.0)
        faces[i] = count
        face_out[i] = count
        coefs[i] = (TIME_STEP * VISC_KV) / (safe * safe)
        push_v[i] = zero
        sum_v[i] = zero

    for c in second:
        c.wait_recv()
    pair = lane // 2
    lev = jnp.where(pair < bank, pair + bank * (lane % 2), n_lev).astype(F32)

    def column(ref, count):
        return jnp.where(lev < count, ref, 0.0)

    u_w = column(rc_w[0], xp[KU, mid, at_w])
    v_w = column(rc_w[1], xp[KV, mid, at_w])
    u_e = column(rc_e[0], xp[KU, mid, at_e])
    v_e = column(rc_e[1], xp[KV, mid, at_e])
    u_last = column(sc_e[0], xp[KU, mid, nx - 1:nx])
    v_zero = column(sc_w[1], xp[KV, mid, FIRST])
    corner_u = jnp.where(lev[FIRST] < xp[KU, at_n, at_w], rc_nw[FIRST, :], 0.0)
    q_e = scaled((u_last + u_e) * (u_last + u_e)) + rp_e[...]
    c_w = scaled((u_w + shift_north(u_w, corner_u)) * (v_w + v_zero))
    hc[0, 0], hc[0, 1] = merged(u_w, q_e)
    hc[1, 0], hc[1, 1] = merged(c_w, v_e)
    corner_p[...] = jnp.where(lev[:SUB] < xp[KV, H - SUB:H, at_e], rc_se[...], 0.0)

    def forces(k, slot):
        kf = k.astype(F32)
        u = jnp.where(kf < faces[0], ub[k], 0.0)
        v = jnp.where(kf < faces[1], vb[k], 0.0)
        p = pp[k]
        b, m = slot_of(k, bank)
        rows_n, rows_s = rr_n[k], rr_s[k]
        u_n = jnp.where(kf < xp[KU, at_n, cols], rows_n[FIRST], 0.0)
        v_n = jnp.where(kf < xp[KV, at_n, cols], rows_n[SECOND], 0.0)
        u_s = jnp.where(kf < xp[KU, at_s, cols], rows_s[FIRST], 0.0)
        v_s = jnp.where(kf < xp[KV, at_s, cols], rows_s[SECOND], 0.0)
        corner_v = turn(corner_p[...], LAST - m - b)[SUB - 1:]
        v_s8 = jnp.broadcast_to(v_s, (SUB, nx))
        v_s_e = shift_east(v_s8, jnp.broadcast_to(corner_v, (SUB, LANES)))[FIRST]
        for i in range(2):
            s_edge[slot, i] = turn(hc[i, b], LANES - m)
        cen_u = shift_west(u, s_edge[slot, 0]) + u
        s_head[slot] = scaled(cen_u * cen_u) + p
        corner = scaled((u + shift_north(u, u_n)) * (v + shift_east(v, s_edge[slot, 1])))
        s_corner[slot] = corner
        corner_s = scaled((u_s + u[first_row]) * (v_s + v_s_e))
        s_side[slot, 0] = corner - shift_south(corner, corner_s)
        cen_v = shift_south(v, v_s) + v
        head_v = scaled(cen_v * cen_v) + p
        edge_v = v[last_row] + v_n
        edge_v = scaled(edge_v * edge_v) + rp_n[k]
        s_side[slot, 1] = (shift_north(head_v, edge_v) - head_v) + corner
        s_now[slot, 0] = u
        s_now[slot, 1] = v

    def solve_down(k, slot):
        kf = k.astype(F32)
        head, corner = s_head[slot], s_corner[slot]
        grad_u = (shift_east(head, s_edge[slot, 0]) - head) + s_side[slot, 0]
        grad_v = s_side[slot, 1] - shift_west(corner, s_edge[slot, 1])
        for f, grad, part, gain in ((0, grad_u, pu, gu), (1, grad_v, pv, gv)):
            count, coef = faces[f], coefs[f]
            wet = kf < count
            up = jnp.where(kf + 1.0 < count, coef, 0.0)
            inv = reduced(1.0 + up + coef * (1.0 - gain[k]))
            gain[k + 1] = up * inv
            pull = jnp.where(wet, grad, 0.0)
            push_v[f] += pull
            low = jnp.where(wet, coef, 0.0)
            part[k + 1] = ((s_now[slot, f] - pull) + low * part[k]) * inv

    def momentum_levels(i, carry):
        k = UN * i
        for d in range(UN):
            forces(jnp.minimum(k + d + 1, n_lev - 1), (d + 1) % UN)
            solve_down(k + d, d)
        return carry

    forces(jnp.int32(0), 0)
    lax.fori_loop(0, n_lev // UN, momentum_levels, 0)

    for f in range(2):
        ext[(FX + f, *own)] = xp[(DZU + f, *own)] * push_v[f] * (-1.0 / TIME_STEP)
        pack(FX + f)
    third = wide_copies(FX, 2)

    def upward(levels):
        def group_of(i, carry):
            levels(n_lev - 1 - i * UE)
            return carry

        lax.fori_loop(0, n_lev // UE, group_of, 0)

    def mix_levels(k0):
        t, s = tb[k0 + 2], sb[k0 + 2]
        for d in range(UE):
            k = k0 - d
            g = gc[k + 1]
            t = tb[k + 1] + g * t
            s = sb[k + 1] + g * s
            tb[k + 1] = t
            sb[k + 1] = s
            gather(t, s, k, bank_ts, tr_s, tr_n)

    upward(mix_levels)
    for i in range(2):
        tc_w[i], tc_e[i] = split_banks(bank_ts.at[i])
    tracer = started([
        remote(tc_w, qc_e, "w"),
        remote(tc_e, qc_w, "e"),
        remote(tr_n, qr_s, "n"),
        remote(tr_s, qr_n, "s"),
    ])

    def rise_levels(k0):
        u, v = pu[k0 + 2], pv[k0 + 2]
        sum_u, sum_w = sum_v[0], sum_v[1]
        for d in range(UE):
            k = k0 - d
            u = pu[k + 1] + gu[k + 1] * u
            v = pv[k + 1] + gv[k + 1] * v
            pu[k + 1] = u
            pv[k + 1] = v
            sum_u += u
            sum_w += v
            b, m = slot_of(k, bank)
            pltpu.store(su_e, turn(u[:, nx - LANES:], m + b + 1), mask=lane == m + b)
            sv_n[k] = v[last_row]
        sum_v[0], sum_v[1] = sum_u, sum_w

    upward(rise_levels)
    fourth = started([remote(su_e, ru_w, "e"), remote(sv_n, rv_s, "n")])

    for c in third:
        c.wait_recv()
    for f in range(2):
        unpack(FX + f)
        xp[BU + f] = jnp.where(xp[KU + f] > 0, dt_sub * ext[FX + f], 0.0)
    xp[BW] = pltpu.roll(xp[BU], 1, 1)
    acc[...] = jnp.zeros(acc.shape, F32)
    norm = 6.0 / (n_sub * (n_sub + 1) * (n_sub + 2))
    line8 = iota((SUB, wide), 0)
    t0 = H // SUB - 1

    def substep(n, lo, hi):
        tide_u, tide_v = tide[0, n], tide[1, n]
        weight = norm * ((n + 1) * (n_sub - n)).astype(F32)

        def finish(t, eta, rolled, rolled_next, u, u_w, v):
            rows = slice(SUB * t, SUB * t + SUB)
            eta_n = jnp.where(line8 == SUB - 1, rolled_next, rolled)
            eta_e = pltpu.roll(eta, wide - 1, 1)
            eta_w = pltpu.roll(eta, 1, 1)
            xp[UW, rows] = u_w + (xp[GW, rows] * (tide_u + (eta_w - eta)) + xp[BW, rows])
            u_new = u + (xp[GU, rows] * (tide_u + (eta - eta_e)) + xp[BU, rows])
            v_new = v + (xp[GV, rows] * (tide_v + (eta - eta_n)) + xp[BV, rows])
            ext[TU, rows] = u_new
            ext[TV, rows] = v_new
            if t0 <= t < (H + ny) // SUB:
                at = slice(SUB * (t - t0), SUB * (t - t0) + SUB)
                acc[0, at] += weight * u_new
                acc[1, at, :nx] += weight * v_new[:, :nx]

        last = None
        v_below = jnp.zeros((SUB, wide), F32)
        for t in range(lo, hi):
            rows = slice(SUB * t, SUB * t + SUB)
            u, u_w, v = ext[TU, rows], xp[UW, rows], ext[TV, rows]
            v_roll = pltpu.roll(v, 1, 0)
            v_s = jnp.where(line8 == 0, v_below, v_roll)
            v_below = v_roll
            eta = ext[ETA, rows] - xp[WD, rows] * ((u - u_w) + (v - v_s))
            ext[ETA, rows] = eta
            rolled = pltpu.roll(eta, SUB - 1, 0)
            if last is not None:
                eta_b, rolled_b, *face_b = last
                finish(t - 1, eta_b, rolled_b, rolled, *face_b)
            last = (eta, rolled, u, u_w, v)
        finish(hi - 1, eta, rolled, rolled, u, u_w, v)

    edge_tiles = H // SUB
    for e in range(edge_tiles, 0, -1):
        begin = max(0, n_sub + 1 - SUB * e) if e < edge_tiles else 0
        end = n_sub + 1 - SUB * (e - 1) if e > 1 else n_sub
        span = (edge_tiles - e, whole // SUB - edge_tiles + e)

        def two(i, carry, begin=begin, span=span):
            substep(begin + 2 * i, *span)
            substep(begin + 2 * i + 1, *span)
            return carry

        lax.fori_loop(0, (end - begin) // 2, two, 0)
        if (end - begin) % 2:
            substep(jnp.int32(end - 1), *span)

    for i in range(3):
        bar_out[i] = ext[(ETA + i, *own)]

    def safe_depth(f, rows, lanes):
        depth = xp[KU + f, rows, lanes] * xp[DZU + f, rows, lanes]
        return jnp.where(depth > 0, depth, 1.0)

    inner = slice(SUB, SUB + ny)
    for f in range(2):
        corr_out[f] = (acc[f, inner, cols] - xp[DZU + f, mid, cols] * sum_v[f]) / safe_depth(f, mid, cols)
    for c in fourth:
        c.wait_recv()
    star = ru_w[...]
    fix = (acc[0, inner, at_w] - xp[DZU, mid, at_w] * jnp.sum(star, axis=1, keepdims=True)) / safe_depth(0, mid, at_w)
    u_c = column(star + fix, xp[KU, mid, at_w])
    star = rv_s[...]
    fix = (acc[1, SUB - 1:SUB, cols] - xp[DZV, at_s, cols] * jnp.sum(star, axis=0)) / safe_depth(1, at_s, cols)
    levels = iota(star.shape, 0).astype(F32)
    vcs_out[...] = jnp.where(levels < xp[KV, at_s, cols][None], star + fix[None], 0.0)
    for c in tracer:
        c.wait_recv()
    for i in range(2):
        halo_out[i, 0], halo_out[i, 1] = merged((0.5 * TIME_STEP) * u_c * (qc_w[i] + tc_w[i]), qc_e[i])
    trow_n_out[...] = qr_n[...]
    trow_s_out[...] = qr_s[...]
    for c in second + third + tracer + fourth:
        c.wait_send()


def last_kernel(us, vs, tm, sm, bar, corr, faces, vcs, halo, trow_n, trow_s,
                eta_out, tu_out, tv_out, u_out, v_out, t_out, s_out,
                new_u, new_v, new_t, new_s, flux, rest, turned, bar_sem, out_sem, *, bank):
    n_lev = u_out.shape[0]
    planes = [pltpu.make_async_copy(bar.at[i], ref, bar_sem.at[i]) for i, ref in enumerate((eta_out, tu_out, tv_out))]
    for c in planes:
        c.start()

    def fluxes(k, slot):
        kf = k.astype(F32)
        u = jnp.where(kf < faces[0], us[k + 1] + corr[0], 0.0)
        v = jnp.where(kf < faces[1], vs[k + 1] + corr[1], 0.0)
        new_u[k] = u
        new_v[k] = v
        u = (0.5 * TIME_STEP) * u
        v = (0.5 * TIME_STEP) * v
        v_s = (0.5 * TIME_STEP) * vcs[k]
        rows_n, rows_s = trow_n[k], trow_s[k]
        b, m = slot_of(k, bank)
        for a, src in ((0, tm), (1, sm)):
            x = src[k + 1]
            turned[slot, a] = turn(halo[a, b], LANES - m)
            flux_x = u * (x + shift_east(x, turned[slot, a]))
            flux_y = v * (x + shift_north(x, rows_n[a:a + 1]))
            edge_y = v_s * (rows_s[a:a + 1] + x[FIRST])
            flux[slot, a] = flux_x
            rest[slot, a] = (x - flux_x) - (flux_y - shift_south(flux_y, edge_y))

    def finish(k, slot):
        wet = k.astype(F32) < faces[2]
        for a, dst in ((0, new_t), (1, new_s)):
            moved = shift_west(flux[slot, a], turned[slot, a])
            dst[k] = jnp.where(wet, rest[slot, a] + moved, 0.0)

    def copies(c):
        return [pltpu.make_async_copy(src.at[pl.ds(c * KB, KB)], dst.at[pl.ds(c * KB, KB)], out_sem.at[i, c])
                for i, (src, dst) in enumerate(((new_u, u_out), (new_v, v_out), (new_t, t_out), (new_s, s_out)))]

    def chunk(c, carry):
        for d in range(KB):
            fluxes(jnp.minimum(c * KB + d + 1, n_lev - 1), (d + 1) % KB)
            finish(c * KB + d, d)
        for copy in copies(c):
            copy.start()
        return carry

    n_copy = n_lev // KB
    fluxes(jnp.int32(0), 0)
    lax.fori_loop(0, n_copy, chunk, 0)
    for c in range(n_copy):
        for copy in copies(c):
            copy.wait()
    for c in planes:
        c.wait()


def solution(mesh):
    n_cols, n_rows = mesh.shape["col"], mesh.shape["row"]

    def local_step(vel_u, vel_v, value_a11, salinity, sea_level, trans_u, trans_v, bathymetry, kmt_levels, tide_force):
        n_lev, ny, nx = vel_u.shape
        whole, wide = ny + 2 * H, nx + LANES
        n_chunk, bank = n_lev // CH, (n_lev + 1) // 2
        hbm_spec = pl.BlockSpec(memory_space=pltpu.HBM)
        vmem_spec = pl.BlockSpec(memory_space=pltpu.VMEM)
        cube = (n_lev, ny, nx)
        deep = (n_lev + 2, ny, nx)
        column, pair_c, rows1, rows2 = (ny, LANES), (2, ny, LANES), (n_lev, 1, nx), (n_lev, 2, nx)
        banks, two, small, both = (2, 2, ny, LANES), (2, ny, nx), (SUB, LANES), (UN, 2, ny, nx)

        edges = (UN, 2, ny, LANES)

        def sds(*shape):
            return jax.ShapeDtypeStruct(shape, F32)

        def bufs(*shapes):
            return [pltpu.VMEM(shape, F32) for shape in shapes]

        def sems(*shape):
            return pltpu.SemaphoreType.DMA(shape)

        passed = [(3, ny, nx), two, (3, ny, nx), rows1, banks, rows2, rows2]
        *cubes, bar, corr, face, vcs, halo, trow_n, trow_s = pl.pallas_call(
            functools.partial(main_kernel, n_rows, n_cols),
            out_shape=bufs(*[deep] * 4, *passed),
            in_specs=[hbm_spec] * 9 + [pl.BlockSpec(memory_space=pltpu.SMEM)],
            out_specs=[vmem_spec] * (4 + len(passed)),
            scratch_shapes=[
                pltpu.VMEM((ny, nx), jnp.int32),
                *bufs((7, whole, wide), (12, whole, wide), (2, ny + SUB, wide)),
                *bufs(*[(7, 3 * SUB, LANES)] * 2, *[(7, 2 * SUB, LANES)] * 2, *[(7, SUB, LANES)] * 4),
                *bufs(cube, cube, *[deep] * 3, cube, *[(ny, nx)] * 4, two, two, two, two, both, (UN, ny, nx), (UN, ny, nx), both, edges),
                *bufs(banks, banks, pair_c, pair_c, column, pair_c, pair_c, column, small, small, banks, small),
                *bufs(rows2, rows2, rows1, rows2, rows2, rows1),
                *bufs(pair_c, pair_c, rows2, rows2, pair_c, pair_c, rows2, rows2, column, rows1, column, rows1),
                sems(5), sems(4, n_chunk), sems(30), sems(30),
            ],
            compiler_params=pltpu.CompilerParams(collective_id=0, has_side_effects=True, vmem_limit_bytes=44 * 2**20),
        )(kmt_levels, bathymetry, sea_level, trans_u, trans_v, vel_u, vel_v, value_a11, salinity, tide_force.T)

        return pl.pallas_call(
            functools.partial(last_kernel, bank=bank),
            out_shape=[sds(ny, nx)] * 3 + [sds(*cube)] * 4,
            in_specs=[vmem_spec] * (4 + len(passed)),
            out_specs=[hbm_spec] * 7,
            scratch_shapes=[*bufs(*[cube] * 4, both, both, edges), sems(3), sems(4, n_lev // KB)],
            compiler_params=pltpu.CompilerParams(vmem_limit_bytes=18 * 2**20),
        )(*cubes, bar, corr, face, vcs, halo, trow_n, trow_s)

    spec_cube = P(None, "row", "col")
    spec_plane = P("row", "col")
    return jax.shard_map(local_step, mesh=mesh, in_specs=(spec_cube,) * 4 + (spec_plane,) * 5 + (P(None, None),),
                         out_specs=(spec_plane,) * 3 + (spec_cube,) * 4, check_vma=False)
```

time: 69.2 us -> 49.4 us (0.71)
  Pallas kernels: 66.6 us -> 48.6 us
  local copies, waits for them, and re-layouts: 1.37 us -> 0 us
    pallas_call x1, Pallas kernels: 19.9 us -> 8.35 us  [local_step(): pl.pallas_call(functools.partial(last_kernel, bank=bank), out_shape=[sds(...]
    pallas_call x1, Pallas kernels: 46.6 us -> 40.3 us  [local_step(): pl.pallas_call(functools.partial(main_kernel, n_rows, n_cols), out_shape=...]
    unnamed x1 -> x0, local copies, waits for them, and re-layouts: 1.37 us -> none
where the time goes in v1:
time: 49.4 us; the launch traced here: 49.3 us
  Pallas kernels  48.6 us (98%)
  between operations  0.64 us (1%)
    pallas_call x1, Pallas kernels, local_step(): pl.pallas_call(functools.partial(main_kernel, n_rows, n_cols), out_shape=...  40.3 us
    pallas_call x1, Pallas kernels, local_step(): pl.pallas_call(functools.partial(last_kernel, bank=bank), out_shape=[sds(...  8.35 us

profile of v1, /device:TPU:0, one launch (start us, length us, event | category | flops | bytes accessed | tf_op | source)
XLA Modules:
  0.0 49.3 jit_solution(14212726149648203230)
XLA Ops:
  0.6 40.3 %shard_map.153 = (f32[77,48,256]{2,1,0:T(8,128)S(1)}, f32[77,48,256]{2,1,0:T(8,128)S(1)}, f32[77,48,256]{2,1,0:T(8,128)S(1)}, f32[77,48,256]{2,1,0:T(8,128)S(1)}...) custom-call(s32[48,256]{1,0:T(8,128)} %kmt_in.1, ...), custom_call_target="tpu_custom_call" | custom-call | tf_op jit(solution)/shard_map/pallas_call | solution.py:644
  40.9 8.4 %shard_map.154 = (f32[48,256]{1,0:T(8,128)}, f32[48,256]{1,0:T(8,128)}, f32[48,256]{1,0:T(8,128)}, f32[75,48,256]{2,1,0:T(8,128)}, f32[75,48,256]{2,1,0:T(8,128)...) custom-call(f32[77,48,256]{2,1,0:T(8,128)S(1)} %get-tuple-element.18.us, f32[77,48,256]{2,1,0:T(8,128)S(1)} %get-tuple-element.19.vs, ...), custom_call_target="tpu_custom_call" | custom-call | tf_op jit(solution)/shard_map/pallas_call | solution.py:662

commit v2 on v1

--- a/solution.py
+++ b/solution.py
@@ -24,7 +24,7 @@
 HEAD = 0.25 * TIME_STEP
 KMT, DEPTH, ETA, TU, TV, FX, FY = range(7)
 KU, KV, DZU, DZV, GU, GV, BU, BV, WD, GW, BW, UW = range(12)
-FIRST, SECOND = slice(0, 1), slice(1, 2)
+FIRST = slice(0, 1)
 
 
 def iota(shape, axis):
@@ -44,8 +44,12 @@
 
 
 def slot_of(k, bank):
-    b = (k >= bank).astype(jnp.int32)
+    b = int(k >= bank) if isinstance(k, int) else (k >= bank).astype(jnp.int32)
     return b, 2 * (k - b * bank)
+
+
+def real(k):
+    return float(k) if isinstance(k, int) else k.astype(F32)
 
 
 def turn(x, n):
@@ -93,7 +97,7 @@
                 pu, pv, tb, sb, bar_out, corr_out, face_out, vcs_out,
                 halo_out, trow_n_out, trow_s_out,
                 kmt_v, ext, xp, acc, pk_w, pk_e, r_e, r_w, r_ne, r_nw, r_se, r_sw,
-                ub, vb, gc, gu, gv, pp, wet_v, dz_v, cc_v, cum_v, faces, coefs, push_v, sum_v, s_now, s_head, s_corner, s_side, s_edge,
+                ub, vb, gc, gu, gv, pp, wet_v, dz_v, cc_v, cum_v, faces, coefs, push_v, sum_v, s_now, s_low, s_head, s_corner, s_side, s_edge, row_h, corner_r,
                 bank_uv, bank_ts, sc_w, sc_e, sp_w, rc_e, rc_w, rp_e, rc_nw, rc_se, hc, corner_p,
                 sr_n, sr_s, sp_s, rr_n, rr_s, rp_n,
                 tc_w, tc_e, tr_n, tr_s, qc_e, qc_w, qr_n, qr_s, su_e, sv_n, ru_w, rv_s,
@@ -101,7 +105,7 @@
     n_sub = tide.shape[1]
     n_lev = u_in.shape[0]
     n_chunk = n_lev // CH
-    bank = (n_lev + 1) // 2
+    bank, n_row = (n_lev + 1) // 2, sp_s.shape[0]
     ny, nx = kmt_in.shape
     dt_sub = TIME_STEP / n_sub
     col, row = lax.axis_index("col"), lax.axis_index("row")
@@ -126,11 +130,6 @@
         src, dst, off = ((u_in, ub, 0), (v_in, vb, 0), (t_in, tb, 1), (s_in, sb, 1))[a]
         return pltpu.make_async_copy(src.at[pl.ds(c * CH, CH)], dst.at[pl.ds(c * CH + off, CH)], in_sem.at[a, c])
 
-    for a in (0, 2):
-        for c in range(n_chunk):
-            load(a, c).start()
-            load(a + 1, c).start()
-
     barrier = pltpu.get_barrier_semaphore()
     for c_id, r_id in where_to.values():
         pl.semaphore_signal(barrier, inc=1, device_id={"col": c_id, "row": r_id}, device_id_type=MESH)
@@ -141,13 +140,32 @@
         c_id, r_id = where_to[to]
         i = len(used)
         used.append(i)
-        return pltpu.make_async_remote_copy(src_ref=src, dst_ref=dst, send_sem=send_sem.at[i], recv_sem=recv_sem.at[i],
+        copy = pltpu.make_async_remote_copy(src_ref=src, dst_ref=dst, send_sem=send_sem.at[i], recv_sem=recv_sem.at[i],
                                             device_id={"col": c_id, "row": r_id}, device_id_type=MESH)
+        return copy, to[0]
+
+    below_wall, above_wall = row < n_rows - 1, row > 0
+
+    def sends(copies, act):
+        for copy, to in copies:
+            if to in "ns":
+                pl.when(below_wall if to == "n" else above_wall)(functools.partial(act, copy))
+            else:
+                act(copy)
 
     def started(copies):
-        for c in copies:
-            c.start()
+        sends(copies, lambda c: c.start())
         return copies
+
+    def sent(copies):
+        sends(copies, lambda c: c.wait_send())
+
+    def received(copies):
+        for copy, to in copies:
+            if to in "ns":
+                pl.when(above_wall if to == "n" else below_wall)(copy.wait_recv)
+            else:
+                copy.wait_recv()
 
     def wide_copies(p0, n):
         ps = pl.ds(p0, n)
@@ -194,12 +212,16 @@
 
     for c in planes:
         c.wait()
+    for a in (0, 2):
+        for c in range(n_chunk):
+            load(a, c).start()
+            load(a + 1, c).start()
     kmt = kmt_v[...].astype(F32)
     ext[(KMT, *own)] = kmt
     for p in range(FX):
         pack(p)
     pl.semaphore_wait(barrier, len(where_to))
-    first = wide_copies(KMT, FX)
+    first = wide_copies(KMT, 2)
 
     zero = jnp.zeros((ny, nx), F32)
     for ref in (bank_uv, bank_ts, sp_w, su_e):
@@ -215,10 +237,11 @@
         here = ((lane + 1 - m) & LAST) < 2
         pltpu.store(banks.at[0, b], turn(both_edges(x), m), mask=here)
         pltpu.store(banks.at[1, b], turn(both_edges(y), m), mask=here)
-        rows_s[k, FIRST] = x[first_row]
-        rows_s[k, SECOND] = y[first_row]
-        rows_n[k, FIRST] = x[last_row]
-        rows_n[k, SECOND] = y[last_row]
+        here = pl.ds(k, 1)
+        rows_s[0, here] = x[first_row]
+        rows_s[1, here] = y[first_row]
+        rows_n[0, here] = x[last_row]
+        rows_n[1, here] = y[last_row]
 
     def in_chunks(arrays, levels, step):
         def chunk(c, carry):
@@ -277,11 +300,11 @@
             pp[k] = pres
             b, m = slot_of(k, bank)
             pltpu.store(sp_w, turn(pres[:, :LANES], m + b), mask=lane == m + b)
-            sp_s[k] = pres[first_row]
+            sp_s[pl.ds(k, 1)] = pres[first_row]
         cum_v[...] = cum
 
     in_chunks((2, 3), pressure_levels, UE)
-    second += started([remote(sp_w, rp_e, "w"), remote(sp_s, rp_n, "s")])
+    last_edges = started([remote(sp_w, rp_e, "w"), remote(sp_s, rp_n, "s")])
 
     def down_levels(i, carry):
         k0 = i * UN
@@ -304,15 +327,15 @@
 
     lax.fori_loop(0, n_lev // UN, down_levels, 0)
 
-    for c in first:
-        c.wait()
-    for p in range(FX):
+    sent(first)
+    received(first)
+    for p in (KMT, DEPTH):
         unpack(p)
     line = iota((whole, wide), 0)
     seen = ((line >= H) | (row > 0)) & ((line < H + ny) | (row < n_rows - 1))
     kx = jnp.where(seen, ext[KMT], 0.0)
     ext[KMT] = kx
-    dzx = ext[DEPTH] / jnp.maximum(kx, 1.0)
+    dzx = jnp.where(seen, ext[DEPTH], 0.0) / jnp.maximum(kx, 1.0)
     ku = jnp.minimum(kx, pltpu.roll(kx, wide - 1, 1))
     kv = jnp.minimum(kx, pltpu.roll(kx, whole - 1, 0))
     dzu = 0.5 * (dzx + pltpu.roll(dzx, wide - 1, 1))
@@ -325,10 +348,6 @@
     xp[GV] = jnp.where(kv > 0, dt_sub * (kv * dzv), 0.0)
     xp[WD] = jnp.where(kx > 0, dt_sub, 0.0)
     xp[GW] = pltpu.roll(xp[GU], 1, 1)
-    ext[ETA] = jnp.where(kx > 0, ext[ETA], 0.0)
-    ext[TU] = jnp.where(ku > 0, ext[TU], 0.0)
-    ext[TV] = jnp.where(kv > 0, ext[TV], 0.0)
-    xp[UW] = pltpu.roll(ext[TU], 1, 1)
     face_out[2] = wet_v[...]
     for i in range(2):
         count = xp[(KU + i, *own)]
@@ -339,8 +358,7 @@
         push_v[i] = zero
         sum_v[i] = zero
 
-    for c in second:
-        c.wait_recv()
+    received(second)
     pair = lane // 2
     lev = jnp.where(pair < bank, pair + bank * (lane % 2), n_lev).astype(F32)
 
@@ -354,66 +372,80 @@
     u_last = column(sc_e[0], xp[KU, mid, nx - 1:nx])
     v_zero = column(sc_w[1], xp[KV, mid, FIRST])
     corner_u = jnp.where(lev[FIRST] < xp[KU, at_n, at_w], rc_nw[FIRST, :], 0.0)
-    q_e = scaled((u_last + u_e) * (u_last + u_e)) + rp_e[...]
+    q_e = scaled((u_last + u_e) * (u_last + u_e))
     c_w = scaled((u_w + shift_north(u_w, corner_u)) * (v_w + v_zero))
-    hc[0, 0], hc[0, 1] = merged(u_w, q_e)
     hc[1, 0], hc[1, 1] = merged(c_w, v_e)
     corner_p[...] = jnp.where(lev[:SUB] < xp[KV, H - SUB:H, at_e], rc_se[...], 0.0)
 
+    def corner_levels(i, carry):
+        for d in range(UE):
+            b, m = slot_of(i * UE + d, bank)
+            corner_r[pl.ds(i * UE + d, 1)] = turn(corner_p[...], LAST - m - b)[SUB - 1:]
+        return carry
+
+    lax.fori_loop(0, n_lev // UE, corner_levels, 0)
+    row_lev = iota((n_row, nx), 0).astype(F32)
+
+    def row_of(x, f, at):
+        return jnp.where(row_lev < xp[KU + f, at, cols], x, 0.0)
+
+    v_s = row_of(rr_s[1], 1, at_s)
+    v_last = row_of(sr_n[1], 1, slice(H + ny - 1, H + ny))
+    v_n = row_of(rr_n[1], 1, at_n)
+    row_h[0] = row_of(rr_n[0], 0, at_n)
+    row_h[1] = scaled((row_of(rr_s[0], 0, at_s) + row_of(sr_s[0], 0, slice(H, H + 1))) * (v_s + shift_east(v_s, corner_r[...])))
+    row_h[2] = v_s
+    row_h[3] = scaled((v_last + v_n) * (v_last + v_n))
+    received(last_edges)
+    state = wide_copies(ETA, 3)
+    hc[0, 0], hc[0, 1] = merged(u_w, q_e + rp_e[...])
+    row_h[3] += jnp.where(below_wall, rp_n[...], 0.0)
+
     def forces(k, slot):
-        kf = k.astype(F32)
-        u = jnp.where(kf < faces[0], ub[k], 0.0)
-        v = jnp.where(kf < faces[1], vb[k], 0.0)
+        kf = real(k)
+        k = k if isinstance(k, int) else jnp.minimum(k, n_lev - 1)
+        masked = []
+        for f, ref in ((0, ub), (1, vb)):
+            wet = kf < faces[f]
+            masked.append(jnp.where(wet, ref[k], 0.0))
+            s_now[slot, f] = masked[f]
+            s_low[slot, f] = jnp.where(wet, coefs[f], 0.0)
+        u, v = masked
         p = pp[k]
         b, m = slot_of(k, bank)
-        rows_n, rows_s = rr_n[k], rr_s[k]
-        u_n = jnp.where(kf < xp[KU, at_n, cols], rows_n[FIRST], 0.0)
-        v_n = jnp.where(kf < xp[KV, at_n, cols], rows_n[SECOND], 0.0)
-        u_s = jnp.where(kf < xp[KU, at_s, cols], rows_s[FIRST], 0.0)
-        v_s = jnp.where(kf < xp[KV, at_s, cols], rows_s[SECOND], 0.0)
-        corner_v = turn(corner_p[...], LAST - m - b)[SUB - 1:]
-        v_s8 = jnp.broadcast_to(v_s, (SUB, nx))
-        v_s_e = shift_east(v_s8, jnp.broadcast_to(corner_v, (SUB, LANES)))[FIRST]
+        u_n, corner_s, v_s, edge_v = [row_h[i, pl.ds(k, 1)] for i in range(4)]
         for i in range(2):
             s_edge[slot, i] = turn(hc[i, b], LANES - m)
         cen_u = shift_west(u, s_edge[slot, 0]) + u
         s_head[slot] = scaled(cen_u * cen_u) + p
         corner = scaled((u + shift_north(u, u_n)) * (v + shift_east(v, s_edge[slot, 1])))
         s_corner[slot] = corner
-        corner_s = scaled((u_s + u[first_row]) * (v_s + v_s_e))
         s_side[slot, 0] = corner - shift_south(corner, corner_s)
         cen_v = shift_south(v, v_s) + v
         head_v = scaled(cen_v * cen_v) + p
-        edge_v = v[last_row] + v_n
-        edge_v = scaled(edge_v * edge_v) + rp_n[k]
         s_side[slot, 1] = (shift_north(head_v, edge_v) - head_v) + corner
-        s_now[slot, 0] = u
-        s_now[slot, 1] = v
-
-    def solve_down(k, slot):
+
+    def solve_down(k, slot, below):
         kf = k.astype(F32)
         head, corner = s_head[slot], s_corner[slot]
         grad_u = (shift_east(head, s_edge[slot, 0]) - head) + s_side[slot, 0]
         grad_v = s_side[slot, 1] - shift_west(corner, s_edge[slot, 1])
         for f, grad, part, gain in ((0, grad_u, pu, gu), (1, grad_v, pv, gv)):
-            count, coef = faces[f], coefs[f]
-            wet = kf < count
-            up = jnp.where(kf + 1.0 < count, coef, 0.0)
-            inv = reduced(1.0 + up + coef * (1.0 - gain[k]))
+            low, up = s_low[slot, f], s_low[below, f]
+            inv = reduced(1.0 + up + low * (1.0 - gain[k]))
             gain[k + 1] = up * inv
-            pull = jnp.where(wet, grad, 0.0)
+            pull = jnp.where(kf < faces[f], grad, 0.0)
             push_v[f] += pull
-            low = jnp.where(wet, coef, 0.0)
             part[k + 1] = ((s_now[slot, f] - pull) + low * part[k]) * inv
 
     def momentum_levels(i, carry):
         k = UN * i
         for d in range(UN):
-            forces(jnp.minimum(k + d + 1, n_lev - 1), (d + 1) % UN)
-            solve_down(k + d, d)
+            forces(k + d + 1, (d + 1) % UN)
+            solve_down(k + d, d, (d + 1) % UN)
         return carry
 
-    forces(jnp.int32(0), 0)
+    forces(0, 0)
     lax.fori_loop(0, n_lev // UN, momentum_levels, 0)
 
     for f in range(2):
@@ -462,14 +494,19 @@
             sum_w += v
             b, m = slot_of(k, bank)
             pltpu.store(su_e, turn(u[:, nx - LANES:], m + b + 1), mask=lane == m + b)
-            sv_n[k] = v[last_row]
+            sv_n[pl.ds(k, 1)] = v[last_row]
         sum_v[0], sum_v[1] = sum_u, sum_w
 
     upward(rise_levels)
     fourth = started([remote(su_e, ru_w, "e"), remote(sv_n, rv_s, "n")])
 
-    for c in third:
-        c.wait_recv()
+    sent(state)
+    received(state)
+    for p in (ETA, TU, TV):
+        unpack(p)
+        ext[p] = jnp.where((xp[WD] if p == ETA else xp[KU + p - TU]) > 0, ext[p], 0.0)
+    xp[UW] = pltpu.roll(ext[TU], 1, 1)
+    received(third)
     for f in range(2):
         unpack(FX + f)
         xp[BU + f] = jnp.where(xp[KU + f] > 0, dt_sub * ext[FX + f], 0.0)
@@ -540,23 +577,20 @@
     inner = slice(SUB, SUB + ny)
     for f in range(2):
         corr_out[f] = (acc[f, inner, cols] - xp[DZU + f, mid, cols] * sum_v[f]) / safe_depth(f, mid, cols)
-    for c in fourth:
-        c.wait_recv()
+    received(fourth)
     star = ru_w[...]
     fix = (acc[0, inner, at_w] - xp[DZU, mid, at_w] * jnp.sum(star, axis=1, keepdims=True)) / safe_depth(0, mid, at_w)
     u_c = column(star + fix, xp[KU, mid, at_w])
-    star = rv_s[...]
-    fix = (acc[1, SUB - 1:SUB, cols] - xp[DZV, at_s, cols] * jnp.sum(star, axis=0)) / safe_depth(1, at_s, cols)
-    levels = iota(star.shape, 0).astype(F32)
-    vcs_out[...] = jnp.where(levels < xp[KV, at_s, cols][None], star + fix[None], 0.0)
-    for c in tracer:
-        c.wait_recv()
+    star = row_of(rv_s[...], 1, at_s)
+    total = jnp.sum(star, axis=0, keepdims=True)
+    fix = (acc[1, SUB - 1:SUB, cols] - xp[DZV, at_s, cols] * total) / safe_depth(1, at_s, cols)
+    vcs_out[...] = row_of(star + fix, 1, at_s)
+    received(tracer)
     for i in range(2):
         halo_out[i, 0], halo_out[i, 1] = merged((0.5 * TIME_STEP) * u_c * (qc_w[i] + tc_w[i]), qc_e[i])
-    trow_n_out[...] = qr_n[...]
-    trow_s_out[...] = qr_s[...]
-    for c in second + third + tracer + fourth:
-        c.wait_send()
+    trow_n_out[...] = jnp.where(below_wall, qr_n[...], 0.0)
+    trow_s_out[...] = jnp.where(above_wall, qr_s[...], 0.0)
+    sent(second + last_edges + third + tracer + fourth)
 
 
 def last_kernel(us, vs, tm, sm, bar, corr, faces, vcs, halo, trow_n, trow_s,
@@ -568,22 +602,22 @@
         c.start()
 
     def fluxes(k, slot):
-        kf = k.astype(F32)
+        kf = real(k)
         u = jnp.where(kf < faces[0], us[k + 1] + corr[0], 0.0)
         v = jnp.where(kf < faces[1], vs[k + 1] + corr[1], 0.0)
         new_u[k] = u
         new_v[k] = v
         u = (0.5 * TIME_STEP) * u
         v = (0.5 * TIME_STEP) * v
-        v_s = (0.5 * TIME_STEP) * vcs[k]
-        rows_n, rows_s = trow_n[k], trow_s[k]
+        here = pl.ds(k, 1)
+        v_s = (0.5 * TIME_STEP) * vcs[here]
         b, m = slot_of(k, bank)
         for a, src in ((0, tm), (1, sm)):
             x = src[k + 1]
             turned[slot, a] = turn(halo[a, b], LANES - m)
             flux_x = u * (x + shift_east(x, turned[slot, a]))
-            flux_y = v * (x + shift_north(x, rows_n[a:a + 1]))
-            edge_y = v_s * (rows_s[a:a + 1] + x[FIRST])
+            flux_y = v * (x + shift_north(x, trow_n[a, here]))
+            edge_y = v_s * (trow_s[a, here] + x[FIRST])
             flux[slot, a] = flux_x
             rest[slot, a] = (x - flux_x) - (flux_y - shift_south(flux_y, edge_y))
 
@@ -606,7 +640,7 @@
         return carry
 
     n_copy = n_lev // KB
-    fluxes(jnp.int32(0), 0)
+    fluxes(0, 0)
     lax.fori_loop(0, n_copy, chunk, 0)
     for c in range(n_copy):
         for copy in copies(c):
@@ -626,7 +660,8 @@
         vmem_spec = pl.BlockSpec(memory_space=pltpu.VMEM)
         cube = (n_lev, ny, nx)
         deep = (n_lev + 2, ny, nx)
-        column, pair_c, rows1, rows2 = (ny, LANES), (2, ny, LANES), (n_lev, 1, nx), (n_lev, 2, nx)
+        n_row = n_lev + -n_lev % SUB
+        column, pair_c, rows1, rows2 = (ny, LANES), (2, ny, LANES), (n_row, nx), (2, n_row, nx)
         banks, two, small, both = (2, 2, ny, LANES), (2, ny, nx), (SUB, LANES), (UN, 2, ny, nx)
 
         edges = (UN, 2, ny, LANES)
@@ -650,11 +685,11 @@
                 pltpu.VMEM((ny, nx), jnp.int32),
                 *bufs((7, whole, wide), (12, whole, wide), (2, ny + SUB, wide)),
                 *bufs(*[(7, 3 * SUB, LANES)] * 2, *[(7, 2 * SUB, LANES)] * 2, *[(7, SUB, LANES)] * 4),
-                *bufs(cube, cube, *[deep] * 3, cube, *[(ny, nx)] * 4, two, two, two, two, both, (UN, ny, nx), (UN, ny, nx), both, edges),
+                *bufs(cube, cube, *[deep] * 3, cube, *[(ny, nx)] * 4, two, two, two, two, both, both, (UN, ny, nx), (UN, ny, nx), both, edges, (4, n_row, nx), (n_row, LANES)),
                 *bufs(banks, banks, pair_c, pair_c, column, pair_c, pair_c, column, small, small, banks, small),
                 *bufs(rows2, rows2, rows1, rows2, rows2, rows1),
                 *bufs(pair_c, pair_c, rows2, rows2, pair_c, pair_c, rows2, rows2, column, rows1, column, rows1),
-                sems(5), sems(4, n_chunk), sems(30), sems(30),
+                sems(5), sems(4, n_chunk), sems(38), sems(38),
             ],
             compiler_params=pltpu.CompilerParams(collective_id=0, has_side_effects=True, vmem_limit_bytes=44 * 2**20),
         )(kmt_levels, bathymetry, sea_level, trans_u, trans_v, vel_u, vel_v, value_a11, salinity, tide_force.T)

time: 49.4 us -> 44.2 us (0.89)
  Pallas kernels: 48.6 us -> 43.4 us
    pallas_call x1, Pallas kernels: 40.3 us -> 35.1 us  [local_step(): pl.pallas_call(functools.partial(main_kernel, n_rows, n_cols), out_shape=...]
where the time goes in v2:
time: 44.2 us; the launch traced here: 44.1 us
  Pallas kernels  43.4 us (98%)
  between operations  0.64 us (1%)
    pallas_call x1, Pallas kernels, local_step(): pl.pallas_call(functools.partial(main_kernel, n_rows, n_cols), out_shape=...  35.1 us
    pallas_call x1, Pallas kernels, local_step(): pl.pallas_call(functools.partial(last_kernel, bank=bank), out_shape=[sds(...  8.33 us

profile of v2, /device:TPU:0, one launch (start us, length us, event | category | flops | bytes accessed | tf_op | source)
XLA Modules:
  0.0 44.1 jit_solution(9784260582729691566)
XLA Ops:
  0.6 35.1 %shard_map.153 = (f32[77,48,256]{2,1,0:T(8,128)S(1)}, f32[77,48,256]{2,1,0:T(8,128)S(1)}, f32[77,48,256]{2,1,0:T(8,128)S(1)}, f32[77,48,256]{2,1,0:T(8,128)S(1)}...) custom-call(s32[48,256]{1,0:T(8,128)} %kmt_in.1, ...), custom_call_target="tpu_custom_call" | custom-call | tf_op jit(solution)/shard_map/pallas_call | solution.py:679
  35.7 8.3 %shard_map.154 = (f32[48,256]{1,0:T(8,128)}, f32[48,256]{1,0:T(8,128)}, f32[48,256]{1,0:T(8,128)}, f32[75,48,256]{2,1,0:T(8,128)}, f32[75,48,256]{2,1,0:T(8,128)...) custom-call(f32[77,48,256]{2,1,0:T(8,128)S(1)} %get-tuple-element.18.us, f32[77,48,256]{2,1,0:T(8,128)S(1)} %get-tuple-element.19.vs, ...), custom_call_target="tpu_custom_call" | custom-call | tf_op jit(solution)/shard_map/pallas_call | solution.py:697

commit v3 on v2

--- a/solution.py
+++ b/solution.py
@@ -123,12 +123,15 @@
     planes = [pltpu.make_async_copy(kmt_in, kmt_v, plane_sem.at[KMT])]
     for i, ref in ((DEPTH, bat_in), (ETA, eta_in), (TU, tu_in), (TV, tv_in)):
         planes.append(pltpu.make_async_copy(ref, ext.at[(i, *own)], plane_sem.at[i]))
-    for c in planes:
-        c.start()
-
     def load(a, c):
         src, dst, off = ((u_in, ub, 0), (v_in, vb, 0), (t_in, tb, 1), (s_in, sb, 1))[a]
         return pltpu.make_async_copy(src.at[pl.ds(c * CH, CH)], dst.at[pl.ds(c * CH + off, CH)], in_sem.at[a, c])
+
+    for c in range(n_chunk):
+        load(0, c).start()
+        load(1, c).start()
+    for c in planes:
+        c.start()
 
     barrier = pltpu.get_barrier_semaphore()
     for c_id, r_id in where_to.values():
@@ -210,19 +213,6 @@
             side = jnp.where(group == 0, e_tile, jnp.where(group == n_groups - 1, w_tile, 0.0))
             ext[p, SUB * t:SUB * t + SUB, nx:] = side
 
-    for c in planes:
-        c.wait()
-    for a in (0, 2):
-        for c in range(n_chunk):
-            load(a, c).start()
-            load(a + 1, c).start()
-    kmt = kmt_v[...].astype(F32)
-    ext[(KMT, *own)] = kmt
-    for p in range(FX):
-        pack(p)
-    pl.semaphore_wait(barrier, len(where_to))
-    first = wide_copies(KMT, 2)
-
     zero = jnp.zeros((ny, nx), F32)
     for ref in (bank_uv, bank_ts, sp_w, su_e):
         ref[...] = jnp.zeros(ref.shape, F32)
@@ -243,10 +233,13 @@
         rows_n[0, here] = x[last_row]
         rows_n[1, here] = y[last_row]
 
-    def in_chunks(arrays, levels, step):
+    def in_chunks(arrays, levels, step, follow=()):
         def chunk(c, carry):
             for a in arrays:
                 load(a, c).wait()
+            if follow:
+                for a in follow:
+                    load(a, c).start()
 
             def group_of(i, carry):
                 levels(c * CH + i * step)
@@ -260,7 +253,7 @@
         for d in range(UE):
             gather(ub[k0 + d], vb[k0 + d], k0 + d, bank_uv, sr_s, sr_n)
 
-    in_chunks((0, 1), edge_levels, UE)
+    in_chunks((0, 1), edge_levels, UE, (2, 3))
 
     def split_banks(banks):
         a, b = banks[0], turn(banks[1], 1)
@@ -268,6 +261,14 @@
 
     for i in range(2):
         sc_w[i], sc_e[i] = split_banks(bank_uv.at[i])
+    for c in planes:
+        c.wait()
+    kmt = kmt_v[...].astype(F32)
+    ext[(KMT, *own)] = kmt
+    for p in range(FX):
+        pack(p)
+    pl.semaphore_wait(barrier, len(where_to))
+    first = wide_copies(KMT, 2)
     second = started([
         remote(sc_w, rc_e, "w"),
         remote(sc_e, rc_w, "e"),
@@ -417,10 +418,11 @@
         for i in range(2):
             s_edge[slot, i] = turn(hc[i, b], LANES - m)
         cen_u = shift_west(u, s_edge[slot, 0]) + u
-        s_head[slot] = scaled(cen_u * cen_u) + p
+        head = scaled(cen_u * cen_u) + p
+        s_head[slot] = head
         corner = scaled((u + shift_north(u, u_n)) * (v + shift_east(v, s_edge[slot, 1])))
         s_corner[slot] = corner
-        s_side[slot, 0] = corner - shift_south(corner, corner_s)
+        s_side[slot, 0] = (corner - shift_south(corner, corner_s)) - head
         cen_v = shift_south(v, v_s) + v
         head_v = scaled(cen_v * cen_v) + p
         s_side[slot, 1] = (shift_north(head_v, edge_v) - head_v) + corner
@@ -428,7 +430,7 @@
     def solve_down(k, slot, below):
         kf = k.astype(F32)
         head, corner = s_head[slot], s_corner[slot]
-        grad_u = (shift_east(head, s_edge[slot, 0]) - head) + s_side[slot, 0]
+        grad_u = shift_east(head, s_edge[slot, 0]) + s_side[slot, 0]
         grad_v = s_side[slot, 1] - shift_west(corner, s_edge[slot, 1])
         for f, grad, part, gain in ((0, grad_u, pu, gu), (1, grad_v, pv, gv)):
             low, up = s_low[slot, f], s_low[below, f]
@@ -632,16 +634,22 @@
                 for i, (src, dst) in enumerate(((new_u, u_out), (new_v, v_out), (new_t, t_out), (new_s, s_out)))]
 
     def chunk(c, carry):
-        for d in range(KB):
-            fluxes(jnp.minimum(c * KB + d + 1, n_lev - 1), (d + 1) % KB)
-            finish(c * KB + d, d)
-        for copy in copies(c):
-            copy.start()
+        def done(d):
+            finish(c * UE + d, d)
+            if d % KB == KB - 1:
+                for copy in copies(c * (UE // KB) + d // KB):
+                    copy.start()
+
+        for d in range(1, UE):
+            fluxes(c * UE + d, d)
+            done(d - 1)
+        fluxes(jnp.minimum(c * UE + UE, n_lev - 1), 0)
+        done(UE - 1)
         return carry
 
     n_copy = n_lev // KB
     fluxes(0, 0)
-    lax.fori_loop(0, n_copy, chunk, 0)
+    lax.fori_loop(0, n_lev // UE, chunk, 0)
     for c in range(n_copy):
         for copy in copies(c):
             copy.wait()
@@ -699,8 +707,8 @@
             out_shape=[sds(ny, nx)] * 3 + [sds(*cube)] * 4,
             in_specs=[vmem_spec] * (4 + len(passed)),
             out_specs=[hbm_spec] * 7,
-            scratch_shapes=[*bufs(*[cube] * 4, both, both, edges), sems(3), sems(4, n_lev // KB)],
-            compiler_params=pltpu.CompilerParams(vmem_limit_bytes=18 * 2**20),
+            scratch_shapes=[*bufs(*[cube] * 4, (UE, 2, ny, nx), (UE, 2, ny, nx), (UE, 2, ny, LANES)), sems(3), sems(4, n_lev // KB)],
+            compiler_params=pltpu.CompilerParams(vmem_limit_bytes=24 * 2**20),
         )(*cubes, bar, corr, face, vcs, halo, trow_n, trow_s)
 
     spec_cube = P(None, "row", "col")

time: 44.2 us -> 43 us (0.973)
  Pallas kernels: 43.4 us -> 41.9 us
    pallas_call x1, Pallas kernels: 35.1 us -> 34.1 us  [local_step(): pl.pallas_call(functools.partial(main_kernel, n_rows, n_cols), out_shape=...]
    pallas_call x1, Pallas kernels: 8.33 us -> 7.82 us  [local_step(): pl.pallas_call(functools.partial(last_kernel, bank=bank), out_shape=[sds(...]
where the time goes in v3:
time: 43 us; the launch traced here: 42.5 us
  Pallas kernels  41.9 us (97%)
  between operations  0.64 us (1%)
    pallas_call x1, Pallas kernels, local_step(): pl.pallas_call(functools.partial(main_kernel, n_rows, n_cols), out_shape=...  34.1 us
    pallas_call x1, Pallas kernels, local_step(): pl.pallas_call(functools.partial(last_kernel, bank=bank), out_shape=[sds(...  7.82 us

profile of v3, /device:TPU:0, one launch (start us, length us, event | category | flops | bytes accessed | tf_op | source)
XLA Modules:
  0.0 42.5 jit_solution(11232783319714554046)
XLA Ops:
  0.6 34.1 %shard_map.153 = (f32[77,48,256]{2,1,0:T(8,128)S(1)}, f32[77,48,256]{2,1,0:T(8,128)S(1)}, f32[77,48,256]{2,1,0:T(8,128)S(1)}, f32[77,48,256]{2,1,0:T(8,128)S(1)}...) custom-call(s32[48,256]{1,0:T(8,128)} %kmt_in.1, ...), custom_call_target="tpu_custom_call" | custom-call | tf_op jit(solution)/shard_map/pallas_call | solution.py:687
  34.7 7.8 %shard_map.154 = (f32[48,256]{1,0:T(8,128)}, f32[48,256]{1,0:T(8,128)}, f32[48,256]{1,0:T(8,128)}, f32[75,48,256]{2,1,0:T(8,128)}, f32[75,48,256]{2,1,0:T(8,128)...) custom-call(f32[77,48,256]{2,1,0:T(8,128)S(1)} %get-tuple-element.18.us, f32[77,48,256]{2,1,0:T(8,128)S(1)} %get-tuple-element.19.vs, ...), custom_call_target="tpu_custom_call" | custom-call | tf_op jit(solution)/shard_map/pallas_call | solution.py:705

commit v4 on v3

--- a/solution.py
+++ b/solution.py
@@ -93,10 +93,10 @@
 
 
 def main_kernel(n_rows, n_cols,
-                kmt_in, bat_in, eta_in, tu_in, tv_in, u_in, v_in, t_in, s_in, tide,
+                kmt_in, bat_in, eta_in, tu_in, tv_in, u_in, v_in, t_in, s_in, tide_in,
                 pu, pv, tb, sb, bar_out, corr_out, face_out, vcs_out,
                 halo_out, trow_n_out, trow_s_out,
-                kmt_v, ext, xp, acc, pk_w, pk_e, r_e, r_w, r_ne, r_nw, r_se, r_sw,
+                tide, kmt_v, ext, xp, acc, pk_w, pk_e, r_e, r_w, r_ne, r_nw, r_se, r_sw,
                 ub, vb, gc, gu, gv, pp, wet_v, dz_v, cc_v, cum_v, faces, coefs, push_v, sum_v, s_now, s_low, s_head, s_corner, s_side, s_edge, row_h, corner_r,
                 bank_uv, bank_ts, sc_w, sc_e, sp_w, rc_e, rc_w, rp_e, rc_nw, rc_se, hc, corner_p,
                 sr_n, sr_s, sp_s, rr_n, rr_s, rp_n,
@@ -123,6 +123,7 @@
     planes = [pltpu.make_async_copy(kmt_in, kmt_v, plane_sem.at[KMT])]
     for i, ref in ((DEPTH, bat_in), (ETA, eta_in), (TU, tu_in), (TV, tv_in)):
         planes.append(pltpu.make_async_copy(ref, ext.at[(i, *own)], plane_sem.at[i]))
+    planes.append(pltpu.make_async_copy(tide_in, tide, plane_sem.at[FX]))
     def load(a, c):
         src, dst, off = ((u_in, ub, 0), (v_in, vb, 0), (t_in, tb, 1), (s_in, sb, 1))[a]
         return pltpu.make_async_copy(src.at[pl.ds(c * CH, CH)], dst.at[pl.ds(c * CH + off, CH)], in_sem.at[a, c])
@@ -265,7 +266,7 @@
         c.wait()
     kmt = kmt_v[...].astype(F32)
     ext[(KMT, *own)] = kmt
-    for p in range(FX):
+    for p in (KMT, DEPTH):
         pack(p)
     pl.semaphore_wait(barrier, len(where_to))
     first = wide_copies(KMT, 2)
@@ -376,15 +377,10 @@
     q_e = scaled((u_last + u_e) * (u_last + u_e))
     c_w = scaled((u_w + shift_north(u_w, corner_u)) * (v_w + v_zero))
     hc[1, 0], hc[1, 1] = merged(c_w, v_e)
-    corner_p[...] = jnp.where(lev[:SUB] < xp[KV, H - SUB:H, at_e], rc_se[...], 0.0)
-
-    def corner_levels(i, carry):
-        for d in range(UE):
-            b, m = slot_of(i * UE + d, bank)
-            corner_r[pl.ds(i * UE + d, 1)] = turn(corner_p[...], LAST - m - b)[SUB - 1:]
-        return carry
-
-    lax.fori_loop(0, n_lev // UE, corner_levels, 0)
+    corner = jnp.where(lev[FIRST] < xp[KV, H - 1:H, at_e], rc_se[SUB - 1:], 0.0)
+    corner_p[...] = jnp.transpose(jnp.broadcast_to(corner, (LANES, LANES)))
+    corner_r[0:bank] = corner_p[pl.ds(0, bank, stride=2)]
+    corner_r[bank:n_lev] = corner_p[pl.ds(1, n_lev - bank, stride=2)]
     row_lev = iota((n_row, nx), 0).astype(F32)
 
     def row_of(x, f, at):
@@ -398,6 +394,8 @@
     row_h[2] = v_s
     row_h[3] = scaled((v_last + v_n) * (v_last + v_n))
     received(last_edges)
+    for p in (ETA, TU, TV):
+        pack(p)
     state = wide_copies(ETA, 3)
     hc[0, 0], hc[0, 1] = merged(u_w, q_e + rp_e[...])
     row_h[3] += jnp.where(below_wall, rp_n[...], 0.0)
@@ -629,9 +627,11 @@
             moved = shift_west(flux[slot, a], turned[slot, a])
             dst[k] = jnp.where(wet, rest[slot, a] + moved, 0.0)
 
+    results = (new_u, u_out), (new_v, v_out), (new_t, t_out), (new_s, s_out)
+
     def copies(c):
-        return [pltpu.make_async_copy(src.at[pl.ds(c * KB, KB)], dst.at[pl.ds(c * KB, KB)], out_sem.at[i, c])
-                for i, (src, dst) in enumerate(((new_u, u_out), (new_v, v_out), (new_t, t_out), (new_s, s_out)))]
+        return [pltpu.make_async_copy(src.at[pl.ds(c * KB, KB)], dst.at[pl.ds(c * KB, KB)], out_sem.at[i])
+                for i, (src, dst) in enumerate(results)]
 
     def chunk(c, carry):
         def done(d):
@@ -647,12 +647,10 @@
         done(UE - 1)
         return carry
 
-    n_copy = n_lev // KB
     fluxes(0, 0)
     lax.fori_loop(0, n_lev // UE, chunk, 0)
-    for c in range(n_copy):
-        for copy in copies(c):
-            copy.wait()
+    for i, (src, dst) in enumerate(results):
+        pltpu.make_async_copy(src, dst, out_sem.at[i]).wait()
     for c in planes:
         c.wait()
 
@@ -687,17 +685,18 @@
         *cubes, bar, corr, face, vcs, halo, trow_n, trow_s = pl.pallas_call(
             functools.partial(main_kernel, n_rows, n_cols),
             out_shape=bufs(*[deep] * 4, *passed),
-            in_specs=[hbm_spec] * 9 + [pl.BlockSpec(memory_space=pltpu.SMEM)],
+            in_specs=[hbm_spec] * 10,
             out_specs=[vmem_spec] * (4 + len(passed)),
             scratch_shapes=[
+                pltpu.SMEM(tide_force.shape[::-1], F32),
                 pltpu.VMEM((ny, nx), jnp.int32),
                 *bufs((7, whole, wide), (12, whole, wide), (2, ny + SUB, wide)),
                 *bufs(*[(7, 3 * SUB, LANES)] * 2, *[(7, 2 * SUB, LANES)] * 2, *[(7, SUB, LANES)] * 4),
                 *bufs(cube, cube, *[deep] * 3, cube, *[(ny, nx)] * 4, two, two, two, two, both, both, (UN, ny, nx), (UN, ny, nx), both, edges, (4, n_row, nx), (n_row, LANES)),
-                *bufs(banks, banks, pair_c, pair_c, column, pair_c, pair_c, column, small, small, banks, small),
+                *bufs(banks, banks, pair_c, pair_c, column, pair_c, pair_c, column, small, small, banks, (LANES, LANES)),
                 *bufs(rows2, rows2, rows1, rows2, rows2, rows1),
                 *bufs(pair_c, pair_c, rows2, rows2, pair_c, pair_c, rows2, rows2, column, rows1, column, rows1),
-                sems(5), sems(4, n_chunk), sems(38), sems(38),
+                sems(6), sems(4, n_chunk), sems(38), sems(38),
             ],
             compiler_params=pltpu.CompilerParams(collective_id=0, has_side_effects=True, vmem_limit_bytes=44 * 2**20),
         )(kmt_levels, bathymetry, sea_level, trans_u, trans_v, vel_u, vel_v, value_a11, salinity, tide_force.T)
@@ -707,7 +706,7 @@
             out_shape=[sds(ny, nx)] * 3 + [sds(*cube)] * 4,
             in_specs=[vmem_spec] * (4 + len(passed)),
             out_specs=[hbm_spec] * 7,
-            scratch_shapes=[*bufs(*[cube] * 4, (UE, 2, ny, nx), (UE, 2, ny, nx), (UE, 2, ny, LANES)), sems(3), sems(4, n_lev // KB)],
+            scratch_shapes=[*bufs(*[cube] * 4, (UE, 2, ny, nx), (UE, 2, ny, nx), (UE, 2, ny, LANES)), sems(3), sems(4)],
             compiler_params=pltpu.CompilerParams(vmem_limit_bytes=24 * 2**20),
         )(*cubes, bar, corr, face, vcs, halo, trow_n, trow_s)
 

time: 43 us -> 41.7 us (0.970)
  Pallas kernels: 41.9 us -> 40.9 us
    pallas_call x1, Pallas kernels: 34.1 us -> 33.5 us  [local_step(): pl.pallas_call(functools.partial(main_kernel, n_rows, n_cols), out_shape=...]
    pallas_call x1, Pallas kernels: 7.82 us -> 7.34 us  [local_step(): pl.pallas_call(functools.partial(last_kernel, bank=bank), out_shape=[sds(...]
where the time goes in v4:
time: 41.7 us; the launch traced here: 41.5 us
  Pallas kernels  40.9 us (98%)
  between operations  0.64 us (2%)
    pallas_call x1, Pallas kernels, local_step(): pl.pallas_call(functools.partial(main_kernel, n_rows, n_cols), out_shape=...  33.5 us
    pallas_call x1, Pallas kernels, local_step(): pl.pallas_call(functools.partial(last_kernel, bank=bank), out_shape=[sds(...  7.34 us

profile of v4, /device:TPU:0, one launch (start us, length us, event | category | flops | bytes accessed | tf_op | source)
XLA Modules:
  0.0 41.5 jit_solution(11217976726761383897)
XLA Ops:
  0.6 33.5 %shard_map.153 = (f32[77,48,256]{2,1,0:T(8,128)S(1)}, f32[77,48,256]{2,1,0:T(8,128)S(1)}, f32[77,48,256]{2,1,0:T(8,128)S(1)}, f32[77,48,256]{2,1,0:T(8,128)S(1)}...) custom-call(s32[48,256]{1,0:T(8,128)} %kmt_in.1, ...), custom_call_target="tpu_custom_call" | custom-call | tf_op jit(solution)/shard_map/pallas_call | solution.py:685
  34.2 7.3 %shard_map.154 = (f32[48,256]{1,0:T(8,128)}, f32[48,256]{1,0:T(8,128)}, f32[48,256]{1,0:T(8,128)}, f32[75,48,256]{2,1,0:T(8,128)}, f32[75,48,256]{2,1,0:T(8,128)...) custom-call(f32[77,48,256]{2,1,0:T(8,128)S(1)} %get-tuple-element.18.us, f32[77,48,256]{2,1,0:T(8,128)S(1)} %get-tuple-element.19.vs, ...), custom_call_target="tpu_custom_call" | custom-call | tf_op jit(solution)/shard_map/pallas_call | solution.py:704

commit v5 on v4

--- a/solution.py
+++ b/solution.py
@@ -15,7 +15,8 @@
 MESH = pl.DeviceIdType.MESH
 H = 32
 CH = 15
-UN = 5
+UN = 15
+UD = 5
 UE = 15
 KB = 5
 SUB, LANES = 8, 128
@@ -309,10 +310,10 @@
     last_edges = started([remote(sp_w, rp_e, "w"), remote(sp_s, rp_n, "s")])
 
     def down_levels(i, carry):
-        k0 = i * UN
+        k0 = i * UD
         g, t_up, s_up = gc[k0], tb[k0], sb[k0]
         wet = k0.astype(F32) < wet_v[...]
-        for d in range(UN):
+        for d in range(UD):
             k = k0 + d
             below = (k + 1).astype(F32) < wet_v[...]
             coef = cc_v[...]
@@ -327,7 +328,7 @@
             wet = below
         return carry
 
-    lax.fori_loop(0, n_lev // UN, down_levels, 0)
+    lax.fori_loop(0, n_lev // UD, down_levels, 0)
 
     sent(first)
     received(first)
@@ -698,7 +699,7 @@
                 *bufs(pair_c, pair_c, rows2, rows2, pair_c, pair_c, rows2, rows2, column, rows1, column, rows1),
                 sems(6), sems(4, n_chunk), sems(38), sems(38),
             ],
-            compiler_params=pltpu.CompilerParams(collective_id=0, has_side_effects=True, vmem_limit_bytes=44 * 2**20),
+            compiler_params=pltpu.CompilerParams(collective_id=0, has_side_effects=True, vmem_limit_bytes=46 * 2**20),
         )(kmt_levels, bathymetry, sea_level, trans_u, trans_v, vel_u, vel_v, value_a11, salinity, tide_force.T)
 
         return pl.pallas_call(

time: 41.7 us -> 41.2 us (0.988)
  Pallas kernels: 40.9 us -> 40.4 us
    pallas_call x1, Pallas kernels: 33.5 us -> 33 us  [local_step(): pl.pallas_call(functools.partial(main_kernel, n_rows, n_cols), out_shape=...]
where the time goes in v5:
time: 41.2 us; the launch traced here: 41 us
  Pallas kernels  40.4 us (98%)
  between operations  0.64 us (2%)
    pallas_call x1, Pallas kernels, local_step(): pl.pallas_call(functools.partial(main_kernel, n_rows, n_cols), out_shape=...  33 us
    pallas_call x1, Pallas kernels, local_step(): pl.pallas_call(functools.partial(last_kernel, bank=bank), out_shape=[sds(...  7.34 us

profile of v5, /device:TPU:0, one launch (start us, length us, event | category | flops | bytes accessed | tf_op | source)
XLA Modules:
  0.0 41.0 jit_solution(8005822801683485330)
XLA Ops:
  0.6 33.0 %shard_map.153 = (f32[77,48,256]{2,1,0:T(8,128)S(1)}, f32[77,48,256]{2,1,0:T(8,128)S(1)}, f32[77,48,256]{2,1,0:T(8,128)S(1)}, f32[77,48,256]{2,1,0:T(8,128)S(1)}...) custom-call(s32[48,256]{1,0:T(8,128)} %kmt_in.1, ...), custom_call_target="tpu_custom_call" | custom-call | tf_op jit(solution)/shard_map/pallas_call | solution.py:686
  33.7 7.3 %shard_map.154 = (f32[48,256]{1,0:T(8,128)}, f32[48,256]{1,0:T(8,128)}, f32[48,256]{1,0:T(8,128)}, f32[75,48,256]{2,1,0:T(8,128)}, f32[75,48,256]{2,1,0:T(8,128)...) custom-call(f32[77,48,256]{2,1,0:T(8,128)S(1)} %get-tuple-element.18.us, f32[77,48,256]{2,1,0:T(8,128)S(1)} %get-tuple-element.19.vs, ...), custom_call_target="tpu_custom_call" | custom-call | tf_op jit(solution)/shard_map/pallas_call | solution.py:705
